TPU v7x, 32 devices: a whole 2x2x4 slice. The times are simulated.
32 devices in a mesh: dp: 2 (over x), tp: 16 (over z, y, core).
Axes of the slice: x: 2, y: 2, z: 4, core: 2. Of those that a mesh axis runs over, the one named last changes fastest.
Arguments:
- x_in: bfloat16 [1024, 1024], P('dp'), parts along dimension 0
- tok_pos: int32 [1024], P('dp'), parts along dimension 0
- self_k: bfloat16 [1024, 128, 16, 64], P('dp', None, 'tp'), parts along dimension 0
- self_v: bfloat16 [1024, 128, 16, 64], P('dp', None, 'tp'), parts along dimension 0
- cross_k: bfloat16 [1024, 64, 16, 64], P('dp', None, 'tp'), parts along dimension 0
- cross_v: bfloat16 [1024, 64, 16, 64], P('dp', None, 'tp'), parts along dimension 0
- enc_mask: int32 [1024, 64], P('dp'), parts along dimension 0
- rel_bias: float32 [32, 16], P(None, 'tp')
- w_q: bfloat16 [1024, 1024], P(None, 'tp')
- w_k: bfloat16 [1024, 1024], P(None, 'tp')
- w_v: bfloat16 [1024, 1024], P(None, 'tp')
- w_o: bfloat16 [1024, 1024], P('tp')
- cross_q: bfloat16 [1024, 1024], P(None, 'tp')
- cross_o: bfloat16 [1024, 1024], P('tp')
- w_gate: bfloat16 [1024, 2816], P(None, 'tp')
- w_up: bfloat16 [1024, 2816], P(None, 'tp')
- w_down: bfloat16 [2816, 1024], P('tp')
- norm_self: bfloat16 [1024], replicated
- norm_cross: bfloat16 [1024], replicated
- norm_mlp: bfloat16 [1024], replicated
Outputs:
- output 1: bfloat16 [1024, 1024], P('dp'), parts along dimension 0
- output 2: bfloat16 [1024, 128, 16, 64], P('dp', None, 'tp'), parts along dimension 0
- output 3: bfloat16 [1024, 128, 16, 64], P('dp', None, 'tp'), parts along dimension 0
There are 2 independent parts. A program takes and returns all parts, laid end to end along the dimension named above; an argument that names none is the same for every part.
All inputs are finite; a program needn't handle non-finite values.
Results may differ from a plain program's by a relative error of at most 0.0189546.
Values are sent between devices in bfloat16 or wider.
A program may use at most 1 GiB of HBM per device.

v0:
```python
import math
import jax
import jax.numpy as jnp
from jax import lax
from jax.sharding import PartitionSpec as P

BUCKET_EDGES = tuple(int(math.ceil(16.0 * 8.0 ** (bucket_step / 16.0))) for bucket_step in range(1, 16))
NEG_FILL = -1e30


def rms_norm(values, norm_scale):
    inv_rms = lax.rsqrt(jnp.mean(values * values, axis=-1, keepdims=True) + 1e-6)
    return (values * inv_rms * norm_scale.astype(jnp.float32)).astype(jnp.bfloat16)


def project(normed, weight):
    return jnp.dot(normed, weight, preferred_element_type=jnp.float32).astype(jnp.bfloat16)


def rel_bucket(distance):
    bucket_edges = jnp.array(BUCKET_EDGES, dtype=jnp.int32)
    far_bucket = 16 + jnp.sum((distance[..., None] >= bucket_edges).astype(jnp.int32), axis=-1)
    return jnp.where(distance < 16, distance, far_bucket)


def attend(queries, keys_all, values_all, extra):
    scores = jnp.einsum('bhk,bthk->bht', queries, keys_all, preferred_element_type=jnp.float32) + extra
    probs_bf = jax.nn.softmax(scores, axis=-1).astype(jnp.bfloat16)
    mixed_out = jnp.einsum('bht,bthk->bhk', probs_bf, values_all, preferred_element_type=jnp.float32)
    return mixed_out.astype(jnp.bfloat16)


def self_terms(tok_pos, rel_bias, t_len):
    key_index = jnp.arange(t_len)
    at_pos = (key_index[None, :] == tok_pos[:, None])[:, :, None, None]
    distance = jnp.maximum(tok_pos[:, None] - key_index[None, :], 0)
    bias_rows = jnp.swapaxes(jnp.take(rel_bias, rel_bucket(distance), axis=0), 1, 2)
    causal = (key_index[None, :] <= tok_pos[:, None])[:, None, :]
    return at_pos, jnp.where(causal, bias_rows, NEG_FILL)


def solution(mesh):
    def tp_sum(partial_out):
        return lax.psum(partial_out.astype(jnp.bfloat16), 'tp').astype(jnp.float32)

    def local_layer(x_in, tok_pos, self_k, self_v, cross_k, cross_v, enc_mask, rel_bias, w_q, w_k, w_v, w_o, cross_q, cross_o, w_gate, w_up, w_down, norm_self, norm_cross, norm_mlp):
        row_count, t_len, head_count, head_dim = self_k.shape
        head_shape = (row_count, head_count, head_dim)
        flat_dim = head_count * head_dim
        residual = x_in.astype(jnp.float32)
        normed = rms_norm(residual, norm_self)
        queries = project(normed, w_q).reshape(head_shape)
        new_keys = project(normed, w_k).reshape(head_shape)
        new_values = project(normed, w_v).reshape(head_shape)
        at_pos, self_extra = self_terms(tok_pos, rel_bias, t_len)
        new_self_k = jnp.where(at_pos, new_keys[:, None], self_k)
        new_self_v = jnp.where(at_pos, new_values[:, None], self_v)
        mixed_self = attend(queries, new_self_k, new_self_v, self_extra)
        residual = residual + tp_sum(jnp.dot(mixed_self.reshape(row_count, flat_dim), w_o, preferred_element_type=jnp.float32))
        normed = rms_norm(residual, norm_cross)
        cross_queries = project(normed, cross_q).reshape(head_shape)
        cross_extra = jnp.where(enc_mask[:, None, :] != 0, 0.0, NEG_FILL)
        mixed_cross = attend(cross_queries, cross_k, cross_v, cross_extra)
        residual = residual + tp_sum(jnp.dot(mixed_cross.reshape(row_count, flat_dim), cross_o, preferred_element_type=jnp.float32))
        normed = rms_norm(residual, norm_mlp)
        gate_pre = jnp.dot(normed, w_gate, preferred_element_type=jnp.float32)
        up_pre = jnp.dot(normed, w_up, preferred_element_type=jnp.float32)
        hidden = (jax.nn.gelu(gate_pre, approximate=True) * up_pre).astype(jnp.bfloat16)
        residual = residual + tp_sum(jnp.dot(hidden, w_down, preferred_element_type=jnp.float32))
        return residual.astype(jnp.bfloat16), new_self_k, new_self_v

    cache_spec = P('dp', None, 'tp', None)
    split_cols = P(None, 'tp')
    split_rows = P('tp', None)
    in_specs = (P('dp', None), P('dp'), cache_spec, cache_spec, cache_spec, cache_spec, P('dp', None), split_cols, split_cols, split_cols, split_cols, split_rows, split_cols, split_rows, split_cols, split_cols, split_rows, P(None), P(None), P(None))
    out_specs = (P('dp', None), cache_spec, cache_spec)
    return jax.shard_map(local_layer, mesh=mesh, in_specs=in_specs, out_specs=out_specs, check_vma=False)
```

profile of v0, /device:TPU:0, one launch (start us, length us, event | category | flops | bytes accessed | tf_op | source)
XLA Modules:
  0.0 370.2 jit_solution(16191127615701427071)
XLA Ops:
  7.2 0.0 copy-start
  7.2 0.0 copy-start.1
  7.2 0.0 copy-start.15
  7.2 0.0 all-reduce.4.cloned.1.call-start
  7.2 1.8 fusion.64
  9.1 2.1 fusion.63
  11.2 0.8 iota_compare_fusion.1
  12.0 0.8 subtract_maximum_fusion
  12.8 1.5 fusion.4
  14.3 0.7 convert_element_type.77
  15.0 1.8 convolution_convert_fusion.6
  16.8 0.1 copy.26
  16.9 0.0 copy-done.1
  16.9 0.0 copy-done.15
  16.9 0.0 copy-start.14
  17.0 0.5 convolution_convert_fusion.5
  17.5 0.1 copy.27
  17.6 0.0 copy-done.16
  17.6 0.5 fusion.9
  18.1 0.0 copy-done.14
  18.1 0.5 convert_reduce_fusion
  18.6 11.2 %broadcast_select_fusion.1 = (bf16[512,128,1,64]{1,3,2,0:T(8,128)(2,1)S(1)}, bf16[512,128,1,64]{1,3,2,0:T(8,128)(2,1)S(1)}) fusion(bf16[512,128,1,64]{1,3,2,0:T(8,128)(2,1)} %param.23, pred[512,128]{1,0:T(8,128)(4,1)S(1)} %iota_compare_fusion.1, bf16[512,64]{1,0:T(8,128)(2,1)S(1)} %copy.26, bf16[512,128,1,64]{1,3,2,0:T(8,128)(2,1)} %param.24, ...), kind=kLoop, calls=%fused_computation.7 | loop fusion | flops 8388608 | bytes 33751040 | tf_op jit(solution)/shard_map/jit(_where)/select_n | solution.py:56
  29.8 0.0 copy-start.4
  29.8 0.0 copy-start.5
  29.8 0.0 copy-start.11
  29.8 2.3 fusion.2
  32.1 1.1 copy-done.4
  33.2 0.0 copy-done.11
  33.2 21.0 %fusion.61 = (f32[512]{0:T(512)S(1)}, f32[512,128]{1,0:T(8,128)S(1)}) fusion(f32[512,128]{1,0:T(8,128)S(1)} %bitcast.187, f32[]{:T(128)} %bitcast.62, f32[]{:T(128)} %bitcast.61, f32[]{:T(128)} %bitcast.60, f32[]{:T(128)} %bitcast.59, f32[]{:T(128)} %bitcast.58, f32[]{:T(128)} %bitcast.57, f32[]{:T(128)} %bitcast.56, f32[]{:T(128)} %bitcast.55, f32[]{:T(128)} %bitcast.53, ...), kind=kLoop, calls=%fused_computation.97 | loop fusion | flops 5570048 | bytes 790656 | tf_op jit(solution)/shard_map/reduce_max | solution.py:28
  54.1 0.2 fusion.43
  54.4 0.2 fusion.50
  54.6 0.0 copy-done.5
  54.6 0.0 copy-start.10
  54.6 4.4 %fusion = f32[512,1,64]{2,1,0:T(1,128)S(1)} fusion(bf16[512,128,1,64]{1,3,2,0:T(8,128)(2,1)S(1)} %get-tuple-element.6, bf16[512,128,1]{1,0,2:T(8,128)(2,1)S(1)} %fusion.50), kind=kOutput, calls=%fused_computation | convolution fusion | flops 8388608 | bytes 8650752 | tf_op jit(solution)/shard_map/bht,bthk->bhk/dot_general | solution.py:29
  59.0 0.0 copy-done.10
  59.1 1.4 convolution_convert_fusion.2
  60.5 0.0 all-reduce.4.cloned.1.call-update
  60.5 0.2 all-reduce.6.cloned.1.call-start
  60.7 0.0 copy-done.12
  60.7 96.1 %all-reduce.4.cloned.1.call-done = bf16[512,1024]{1,0:T(8,128)(2,1)} async-done(((bf16[512,1024]{1,0:T(8,128)(2,1)}), bf16[512,1024]{1,0:T(8,128)(2,1)}) %all-reduce.4.cloned.1.call-update) | async-done | bytes 1048592 | tf_op jit(solution)/shard_map/psum | solution.py:44
  156.8 1.7 multiply_reduce_fusion.3
  158.6 0.5 fusion.8
  159.1 0.1 copy.43
  159.2 0.0 copy-start.7
  159.2 0.0 copy-start.6
  159.2 3.7 %multiply_reduce_fusion.1 = f32[512,64]{0,1:T(8,128)S(1)} fusion(f32[512,64]{0,1:T(8,128)S(1)} %copy.43, bf16[512,64,1,64]{0,3,2,1:T(8,128)(2,1)} %param.25), kind=kLoop, calls=%fused_computation.5 | loop fusion | flops 6258688 | bytes 4456448 | tf_op jit(solution)/shard_map/bhk,bthk->bht/dot_general | solution.py:27
  163.0 0.1 fusion.51
  163.1 0.0 copy-done.6
  163.1 0.0 copy-start.9
  163.2 1.1 multiply_reduce_fusion
  164.3 0.1 copy.42
  164.4 0.0 copy-done.9
  164.4 1.4 convolution_convert_fusion.1
  165.8 0.0 all-reduce.6.cloned.1.call-update
  165.8 0.0 all-reduce.8.cloned.1.call-start
  165.9 92.7 %all-reduce.6.cloned.1.call-done = bf16[512,1024]{1,0:T(8,128)(2,1)} async-done(((bf16[512,1024]{1,0:T(8,128)(2,1)}), bf16[512,1024]{1,0:T(8,128)(2,1)}) %all-reduce.6.cloned.1.call-update) | async-done | bytes 1048592 | tf_op jit(solution)/shard_map/psum | solution.py:44
  258.6 1.9 multiply_reduce_fusion.2
  260.5 0.0 copy-start.8
  260.5 1.5 multiply_convert_fusion
  262.0 2.5 fusion.65
  264.4 3.4 convolution_convert_fusion
  267.8 0.0 all-reduce.8.cloned.1.call-update
  267.8 92.8 %all-reduce.8.cloned.1.call-done = bf16[512,1024]{1,0:T(8,128)(2,1)} async-done(((bf16[512,1024]{1,0:T(8,128)(2,1)}), bf16[512,1024]{1,0:T(8,128)(2,1)}) %all-reduce.8.cloned.1.call-update) | async-done | bytes 1048592 | tf_op jit(solution)/shard_map/psum | solution.py:44
  360.6 3.1 add_convert_fusion
  (20 shorter events, 0.1 us)
Async XLA Ops:
  7.2 257.3 %copy-start = (bf16[176,1024]{1,0:T(8,128)(2,1)S(1)}, bf16[176,1024]{1,0:T(8,128)(2,1)}, u32[]{:S(2)}) copy-start(bf16[176,1024]{1,0:T(8,128)(2,1)} %param.37) | copy-start | bytes 1081348
  7.2 9.8 %copy-start.1 = (bf16[512,1024]{1,0:T(8,128)(2,1)S(1)}, bf16[512,1024]{1,0:T(8,128)(2,1)}, u32[]{:S(2)}) copy-start(bf16[512,1024]{1,0:T(8,128)(2,1)} %param.21) | copy-start | bytes 3145732
  7.2 9.7 %copy-start.15 = (bf16[1024,64]{0,1:T(8,128)(2,1)S(1)}, bf16[1024,64]{0,1:T(8,128)(2,1)}, u32[]{:S(2)}) copy-start(bf16[1024,64]{0,1:T(8,128)(2,1)} %param.31) | copy-start | bytes 393220
  7.2 149.6 %all-reduce.4.cloned.1.call-start = ((), (), s32[]{:S(2)}) async-start(), calls=%async_computation | async-start | bytes 2097152 | tf_op jit(solution)/shard_map/psum | solution.py:44
  15.0 2.6 copy-start.16
  16.9 1.2 copy-start.14
  29.8 3.4 copy-start.4
  29.8 24.8 %copy-start.5 = (bf16[512,128,1,64]{1,3,2,0:T(8,128)(2,1)}, bf16[512,128,1,64]{1,3,2,0:T(8,128)(2,1)S(1)}, u32[]{:S(2)}) copy-start(bf16[512,128,1,64]{1,3,2,0:T(8,128)(2,1)S(1)} %get-tuple-element.6) | copy-start | bytes 25165828
  29.8 3.4 copy-start.11
  54.6 4.4 %copy-start.10 = (bf16[64,1024]{1,0:T(8,128)(2,1)S(1)}, bf16[64,1024]{1,0:T(8,128)(2,1)}, u32[]{:S(2)}) copy-start(bf16[64,1024]{1,0:T(8,128)(2,1)} %param.32) | copy-start | bytes 393220
  59.0 1.7 copy-start.12
  59.1 99.5 %copy-start.17 = (bf16[1024,64]{0,1:T(8,128)(2,1)S(1)}, bf16[1024,64]{0,1:T(8,128)(2,1)}, u32[]{:S(2)}) copy-start(bf16[1024,64]{0,1:T(8,128)(2,1)} %param.33) | copy-start | bytes 393220
  60.5 198.1 %all-reduce.6.cloned.1.call-start = ((), (), s32[]{:S(2)}) async-start(), calls=%async_computation.1 | async-start | bytes 2097152 | tf_op jit(solution)/shard_map/psum | solution.py:44
  156.8 1.7 copy-start.2
  159.2 3.8 %copy-start.7 = (s32[512,64]{0,1:T(8,128)S(1)}, s32[512,64]{0,1:T(8,128)}, u32[]{:S(2)}) copy-start(s32[512,64]{0,1:T(8,128)} %param.27) | copy-start | bytes 393220
  159.2 3.9 %copy-start.6 = (bf16[512,64,1,64]{0,3,2,1:T(8,128)(2,1)S(1)}, bf16[512,64,1,64]{0,3,2,1:T(8,128)(2,1)}, u32[]{:S(2)}) copy-start(bf16[512,64,1,64]{0,3,2,1:T(8,128)(2,1)} %param.26) | copy-start | bytes 12582916
  163.1 1.2 copy-start.9
  164.2 1.6 copy-start.13
  165.8 194.8 %all-reduce.8.cloned.1.call-start = ((), (), s32[]{:S(2)}) async-start(), calls=%async_computation.2 | async-start | bytes 2097152 | tf_op jit(solution)/shard_map/psum | solution.py:44
  258.6 1.9 copy-start.3
  260.5 1.5 copy-start.8
Sparse Core Ops, SparseCore 0:
  60.6 96.1 all-reduce.3
  165.9 92.6 all-reduce.5
  267.9 92.6 all-reduce.7
where the time goes:
time: 371 us; the launch traced here: 370 us
  waiting for transfers between devices  282 us (76%)
  other arithmetic  50 us (13%)
  matrix products  18.6 us (5%)
  between operations  14.1 us (4%)
  local copies, waits for them, and re-layouts  5.58 us (2%)
    psum x3, waiting for transfers between devices, tp_sum(): return lax.psum(partial_out.astype(jnp.bfloat16), 'tp').astype(jnp.float32)  282 us
    reduce_max x2, other arithmetic, attend(): probs_bf = jax.nn.softmax(scores, axis=-1).astype(jnp.bfloat16)  21 us
    select_n x1, other arithmetic, local_layer(): new_self_k = jnp.where(at_pos, new_keys[:, None], self_k)  11.2 us
  transfers between devices with their start and end apart: 3, of which 3 were waited for; matrix products, arithmetic and copies ran while one was open for 0% of the time, Pallas kernels for 0%

commit v1 on v0

v1 whole, which is shorter than its diff:
```python
import math
import jax
import jax.numpy as jnp
from jax import lax
from jax.experimental import pallas as pl
from jax.experimental.pallas import tpu as pltpu
from jax.sharding import PartitionSpec as P

BUCKET_EDGES = tuple(range(1, 16)) + (16,) + tuple(int(math.ceil(16.0 * 8.0 ** (m / 16.0))) for m in range(1, 16))
NEG_FILL = -1e30
MESH = pl.DeviceIdType.MESH
F32 = jnp.float32
BF16 = jnp.bfloat16
K_ORDER = (2, 1, 3)


def rms_norm(values, norm_scale):
    inv_rms = lax.rsqrt(jnp.mean(values * values, axis=-1, keepdims=True) + 1e-6)
    return (values * inv_rms * norm_scale.astype(F32)).astype(BF16)


def project(normed, weight):
    return jnp.dot(normed, weight, preferred_element_type=F32).astype(BF16)


def gelu_tanh(u):
    return u * (0.5 * (1.0 + jnp.tanh(math.sqrt(2.0 / math.pi) * (u + 0.044715 * (u * u * u)))))


def dot_nt(a, b):
    return lax.dot_general(a, b, (((1,), (1,)), ((), ())), preferred_element_type=F32)


def dot_nn(a, b):
    return jnp.dot(a, b, preferred_element_type=F32)


def tail_kernel(x_hbm, attn_ref, mask_ref, ck_hbm, cv_hbm, wo_hbm, cq_hbm, co_hbm, wg_hbm, wu_hbm, wd_hbm, nc_ref, nm_ref,
                out_ref,
                x_buf, ck, cv, wo2, cq2, co2, wg2, wu2, wd2, att_in, pair, q_snd, q_all, o_snd, o_rcv, scores,
                y_snd, y_rcv, own, z_snd, z_rcv, h_buf, act,
                loc_sem, w_ssem, w_rsem, ys_sem, yr_sem, zs_sem, zr_sem, gys_sem, gyr_sem, gzs_sem, gzr_sem, cs_sem, cr_sem):
    me = lax.axis_index("tp")
    c = lax.rem(me, 2)
    y = lax.rem(me // 2, 2)
    z = me // 4
    core_peer = {"tp": z * 4 + y * 2 + (1 - c)}
    y_peer = {"tp": z * 4 + (1 - y) * 2 + c}
    z_peer = {k: {"tp": lax.rem(z + k, 4) * 4 + y * 2 + c} for k in (1, 2, 3)}
    my_row = c * 256 + y * 128 + z * 32
    sends = []

    def remote(src, dst, ssem, rsem, peer):
        return pltpu.make_async_remote_copy(src_ref=src, dst_ref=dst, send_sem=ssem, recv_sem=rsem, device_id=peer, device_id_type=MESH)

    def start(src, dst, ssem, rsem, peer):
        copy = remote(src, dst, ssem, rsem, peer)
        copy.start()
        sends.append(copy)
        return copy

    def chunk(base, zz):
        return pl.ds(pl.multiple_of(base + zz * 32, 32), 32)

    half = wg2.shape[0] // 2
    local = [
        pltpu.make_async_copy(x_hbm.at[pl.ds(pl.multiple_of(my_row, 32), 32)], x_buf, loc_sem.at[0]),
        pltpu.make_async_copy(wo_hbm, wo2.at[pl.ds(0, 64)], loc_sem.at[1]),
        pltpu.make_async_copy(cq_hbm, cq2.at[0], loc_sem.at[2]),
        pltpu.make_async_copy(ck_hbm, ck, loc_sem.at[3]),
        pltpu.make_async_copy(cv_hbm, cv, loc_sem.at[4]),
        pltpu.make_async_copy(co_hbm, co2.at[pl.ds(0, 64)], loc_sem.at[5]),
        pltpu.make_async_copy(wg_hbm, wg2.at[pl.ds(0, half)], loc_sem.at[6]),
        pltpu.make_async_copy(wu_hbm, wu2.at[pl.ds(0, half)], loc_sem.at[7]),
        pltpu.make_async_copy(wd_hbm, wd2.at[pl.ds(0, half)], loc_sem.at[8]),
    ]
    for copy in local:
        copy.start()

    barrier = pltpu.get_barrier_semaphore()
    for peer in (core_peer, y_peer, z_peer[1], z_peer[2], z_peer[3]):
        pl.semaphore_signal(barrier, inc=1, device_id=peer, device_id_type=MESH)
    pl.semaphore_wait(barrier, 5)

    att_copy = start(attn_ref.at[pl.ds(pl.multiple_of((1 - c) * 256, 256), 256)], att_in, w_ssem.at[0], w_rsem.at[0], core_peer)
    wo_copy = start(wo_hbm, wo2.at[pl.ds(64, 64)], w_ssem.at[1], w_rsem.at[1], core_peer)
    cq_copy = start(cq_hbm, cq2.at[1], w_ssem.at[2], w_rsem.at[2], core_peer)
    co_copy = start(co_hbm, co2.at[pl.ds(64, 64)], w_ssem.at[3], w_rsem.at[3], core_peer)
    wg_copy = start(wg_hbm, wg2.at[pl.ds(half, half)], w_ssem.at[4], w_rsem.at[4], core_peer)
    wu_copy = start(wu_hbm, wu2.at[pl.ds(half, half)], w_ssem.at[5], w_rsem.at[5], core_peer)
    wd_copy = start(wd_hbm, wd2.at[pl.ds(half, half)], w_ssem.at[6], w_rsem.at[6], core_peer)

    def reduce_scatter(p, partial_of):
        y_snd[p] = partial_of((1 - y) * 128).astype(BF16)
        y_copies = {}
        for k in K_ORDER + (0,):
            zz = lax.rem(z + k, 4)
            y_copies[k] = start(y_snd.at[p, chunk(0, zz)], y_rcv.at[p, k], ys_sem.at[p, k], yr_sem.at[p, k], y_peer)
        own[...] = partial_of(y * 128)
        z_copies = {}
        for k in K_ORDER:
            zz = lax.rem(z + k, 4)
            y_copies[k].wait_recv()
            z_snd[p, k - 1] = (own[chunk(0, zz)] + y_rcv[p, k].astype(F32)).astype(BF16)
            z_copies[k] = start(z_snd.at[p, k - 1], z_rcv.at[p, k - 1], zs_sem.at[p, k - 1], zr_sem.at[p, k - 1], z_peer[k])
        y_copies[0].wait_recv()
        total = own[chunk(0, z)] + y_rcv[p, 0].astype(F32)
        for k in (1, 3, 2):
            z_copies[k].wait_recv()
            total = total + z_rcv[p, k - 1].astype(F32)
        return total

    def gather(p, buf, base):
        mine = buf.at[chunk(base + y * 128, z)]
        start(mine, mine, gys_sem.at[p, 0], gyr_sem.at[p, 0], y_peer)
        for k in K_ORDER:
            start(mine, mine, gzs_sem.at[p, k - 1], gzr_sem.at[p, k - 1], z_peer[k])

    def gathered_z(p, buf, base, k):
        part = buf.at[chunk(base + y * 128, lax.rem(z + 4 - k, 4))]
        remote(part, part, gzs_sem.at[p, k - 1], gzr_sem.at[p, k - 1], z_peer[k]).wait_recv()
        start(part, part, gys_sem.at[p, k], gyr_sem.at[p, k], y_peer)
        return part

    def gathered_y(p, buf, base, k):
        part = buf.at[chunk(base + (1 - y) * 128, lax.rem(z + 4 - k, 4))]
        remote(part, part, gys_sem.at[p, k], gyr_sem.at[p, k], y_peer).wait_recv()
        return part

    pair[:, 0:64] = attn_ref[pl.ds(pl.multiple_of(c * 256, 256), 256), :]
    att_copy.wait_recv()
    pair[:, 64:128] = att_in[...]
    local[1].wait()
    wo_copy.wait_recv()

    def rows_of(base):
        return pl.ds(pl.multiple_of(base, 128), 128)

    total = reduce_scatter(0, lambda base: dot_nn(pair[rows_of(base)], wo2[...]))
    local[0].wait()
    resid = x_buf[...].astype(F32) + total
    h_buf[0, chunk(y * 128, z)] = rms_norm(resid, nc_ref[...])
    gather(0, h_buf.at[0], 0)
    for k in (1, 3, 2):
        gathered_z(0, h_buf.at[0], 0, k)
    for k in (0, 1, 3, 2):
        gathered_y(0, h_buf.at[0], 0, k)

    cq_copy.wait_recv()
    q_snd[...] = dot_nt(cq2[1], h_buf[0]).astype(BF16)
    q_copy = start(q_snd, q_all.at[c], w_ssem.at[7], w_rsem.at[7], core_peer)
    local[2].wait()
    q_all[c] = dot_nt(cq2[0], h_buf[0]).astype(BF16)
    local[3].wait()
    local[4].wait()

    def cross(half_id):
        outs = []
        for block in range(2):
            lanes = pl.ds(pl.multiple_of(half_id * 256 + block * 128, 128), 128)
            q_blk = q_all[half_id, :, block * 128:block * 128 + 128].astype(F32)

            def score_step(i, carry):
                rows = pl.ds(pl.multiple_of(i * 8, 8), 8)
                scores[rows, :] = jnp.sum(ck[rows, :, lanes].astype(F32) * q_blk[None], axis=1)
                return carry

            lax.fori_loop(0, 8, score_step, 0)
            s = scores[...] + jnp.where(mask_ref[:, lanes] != 0, 0.0, NEG_FILL)
            e = jnp.exp(s - jnp.max(s, axis=0, keepdims=True))
            scores[...] = (e / jnp.sum(e, axis=0, keepdims=True)).astype(BF16).astype(F32)

            def mix_step(i, acc):
                rows = pl.ds(pl.multiple_of(i * 8, 8), 8)
                p_blk = scores[rows, :]
                for j in range(8):
                    acc = acc + cv[i * 8 + j, :, lanes].astype(F32) * p_blk[j:j + 1, :]
                return acc

            outs.append(lax.fori_loop(0, 8, mix_step, jnp.zeros((64, 128), F32)).astype(BF16))
        return outs

    mine = cross(c)
    q_in = remote(q_snd, q_all.at[1 - c], w_ssem.at[7], w_rsem.at[7], core_peer)
    q_in.wait_recv()
    theirs = cross(1 - c)
    for block in range(2):
        o_snd[:, block * 128:block * 128 + 128] = theirs[block]
    o_copy = start(o_snd, o_rcv, w_ssem.at[8], w_rsem.at[8], core_peer)
    for block in range(2):
        pair[block * 128:block * 128 + 128, 0:64] = mine[block].astype(F32).T.astype(BF16)
    o_copy.wait_recv()
    pair[:, 64:128] = o_rcv[...].astype(F32).T.astype(BF16)
    local[5].wait()
    co_copy.wait_recv()
    resid = resid + reduce_scatter(1, lambda base: dot_nn(pair[rows_of(base)], co2[...]))
    h_buf[1, chunk(y * 128, z)] = rms_norm(resid, nm_ref[...])
    gather(1, h_buf.at[1], 0)
    for copy in local[6:]:
        copy.wait()
    for copy in (wg_copy, wu_copy, wd_copy):
        copy.wait_recv()
    for k in (1, 3, 2):
        gathered_z(1, h_buf.at[1], 0, k)

    def mlp(base):
        h = h_buf[1, rows_of(base)]
        act[rows_of(base)] = (gelu_tanh(dot_nt(h, wg2[...])) * dot_nt(h, wu2[...])).astype(BF16)

    mlp(y * 128)
    for k in (0, 1, 3, 2):
        gathered_y(1, h_buf.at[1], 0, k)
    mlp((1 - y) * 128)
    resid = resid + reduce_scatter(2, lambda base: dot_nn(act[rows_of(base)], wd2[...]))

    out_ref[pl.ds(pl.multiple_of(my_row, 32), 32)] = resid.astype(BF16)
    gather(2, out_ref, c * 256)
    parts = [out_ref.at[chunk(c * 256 + y * 128, z)]]

    def to_core(part, slot):
        start(part, part, cs_sem.at[slot], cr_sem.at[slot], core_peer)

    to_core(parts[0], 0)
    for k in (1, 3, 2):
        to_core(gathered_z(2, out_ref, c * 256, k), k)
    for k in (0, 1, 3, 2):
        to_core(gathered_y(2, out_ref, c * 256, k), 4 + k)
    for yy in range(2):
        for k in range(4):
            base = (1 - c) * 256 + (y if yy == 0 else 1 - y) * 128
            part = out_ref.at[chunk(base, lax.rem(z + 4 - k, 4))]
            remote(part, part, cs_sem.at[yy * 4 + k], cr_sem.at[yy * 4 + k], core_peer).wait_recv()
    for copy in sends:
        copy.wait_send()


def tail(x_in, attn, mask_t, ck_t, cv_t, wo, cq_t, co, wg_t, wu_t, wd, nc, nm):
    any_spec = pl.BlockSpec(memory_space=pl.ANY)
    vmem = pl.BlockSpec(memory_space=pltpu.VMEM)
    units = wd.shape[0]
    dma = pltpu.SemaphoreType.DMA
    scratch = [
        pltpu.VMEM((32, 1024), BF16), pltpu.VMEM(ck_t.shape, BF16), pltpu.VMEM(cv_t.shape, BF16),
        pltpu.VMEM((128, 1024), BF16), pltpu.VMEM((2, 64, 1024), BF16), pltpu.VMEM((128, 1024), BF16),
        pltpu.VMEM((2 * units, 1024), BF16), pltpu.VMEM((2 * units, 1024), BF16), pltpu.VMEM((2 * units, 1024), BF16),
        pltpu.VMEM((256, 64), BF16), pltpu.VMEM((256, 128), BF16), pltpu.VMEM((64, 256), BF16), pltpu.VMEM((2, 64, 256), BF16),
        pltpu.VMEM((64, 256), BF16), pltpu.VMEM((64, 256), BF16), pltpu.VMEM((64, 128), F32),
        pltpu.VMEM((3, 128, 1024), BF16), pltpu.VMEM((3, 4, 32, 1024), BF16), pltpu.VMEM((128, 1024), F32),
        pltpu.VMEM((3, 3, 32, 1024), BF16), pltpu.VMEM((3, 3, 32, 1024), BF16), pltpu.VMEM((2, 256, 1024), BF16),
        pltpu.VMEM((256, 2 * units), BF16),
        dma((9,)), dma((9,)), dma((9,)), dma((3, 4)), dma((3, 4)), dma((3, 3)), dma((3, 3)),
        dma((3, 4)), dma((3, 4)), dma((3, 3)), dma((3, 3)), dma((8,)), dma((8,)),
    ]
    return pl.pallas_call(
        tail_kernel,
        out_shape=jax.ShapeDtypeStruct(x_in.shape, BF16),
        in_specs=[any_spec, vmem, vmem] + [any_spec] * 8 + [vmem, vmem],
        out_specs=vmem,
        scratch_shapes=scratch,
        compiler_params=pltpu.CompilerParams(collective_id=0, has_side_effects=True, vmem_limit_bytes=40 * 1024 * 1024),
        name="tail",
    )(x_in, attn, mask_t, ck_t, cv_t, wo, cq_t, co, wg_t, wu_t, wd, nc, nm)


def bias_table(rel_bias, t_len):
    distance = jnp.arange(t_len)[:, None] - jnp.arange(t_len)[None, :]
    table = jnp.full((t_len, t_len), rel_bias[0, 0], F32)
    for bucket, edge in enumerate(BUCKET_EDGES):
        table = jnp.where(distance >= edge, rel_bias[bucket + 1, 0], table)
    return table


def solution(mesh):
    def local_layer(x_in, tok_pos, self_k, self_v, cross_k, cross_v, enc_mask, rel_bias, w_q, w_k, w_v, w_o, cross_q, cross_o, w_gate, w_up, w_down, norm_self, norm_cross, norm_mlp):
        row_count, t_len, _, head_dim = self_k.shape
        normed = rms_norm(x_in.astype(F32), norm_self)
        queries = project(normed, w_q)[:, None, :]
        new_keys = project(normed, w_k)[:, None, None, :]
        new_values = project(normed, w_v)[:, None, None, :]
        key_index = jnp.arange(t_len)
        at_pos = key_index[None, :] == tok_pos[:, None]
        bias = jnp.dot(at_pos.astype(F32), bias_table(rel_bias, t_len), precision=lax.Precision.HIGHEST)
        extra = jnp.where(key_index[None, :] <= tok_pos[:, None], bias, NEG_FILL)[:, None, :]
        new_self_k = jnp.where(at_pos[:, :, None, None], new_keys, self_k)
        new_self_v = jnp.where(at_pos[:, :, None, None], new_values, self_v)
        scores = jnp.einsum('bhk,bthk->bht', queries, new_self_k, preferred_element_type=F32) + extra
        probs = jax.nn.softmax(scores, axis=-1).astype(BF16)
        mixed = jnp.einsum('bht,bthk->bhk', probs, new_self_v, preferred_element_type=F32).astype(BF16)
        attn = mixed.reshape(row_count, head_dim)
        ck_t = jnp.transpose(cross_k[:, :, 0, :], (1, 2, 0))
        cv_t = jnp.transpose(cross_v[:, :, 0, :], (1, 2, 0))
        out = tail(x_in, attn, enc_mask.T, ck_t, cv_t, w_o, cross_q.T, cross_o, w_gate.T, w_up.T, w_down,
                   norm_cross[None, :], norm_mlp[None, :])
        return out, new_self_k, new_self_v

    cache_spec = P('dp', None, 'tp', None)
    split_cols = P(None, 'tp')
    split_rows = P('tp', None)
    in_specs = (P('dp', None), P('dp'), cache_spec, cache_spec, cache_spec, cache_spec, P('dp', None), split_cols, split_cols, split_cols, split_cols, split_rows, split_cols, split_rows, split_cols, split_cols, split_rows, P(None), P(None), P(None))
    out_specs = (P('dp', None), cache_spec, cache_spec)
    return jax.shard_map(local_layer, mesh=mesh, in_specs=in_specs, out_specs=out_specs, check_vma=False)
```

time: 371 us -> 144 us (0.39)
  waiting for transfers between devices: 282 us -> 0 us
  Pallas kernels: 0 us -> 81.5 us
  other arithmetic: 50 us -> 15.1 us
  matrix products: 18.6 us -> 34.6 us
  between operations: 14.1 us -> 0.93 us
  local copies, waits for them, and re-layouts: 5.58 us -> 10.4 us
    psum x3 -> x0, waiting for transfers between devices: 282 us -> none  [tp_sum(): return lax.psum(partial_out.astype(jnp.bfloat16), 'tp').astype(jnp.float32)]
    pallas_call x0 -> x1, Pallas kernels: none -> 81.5 us  [tail(): pl.pallas_call(tail_kernel, out_shape=jax.ShapeDtypeStruct(x_in.shape, BF...]
    reduce_max x2 -> x0, other arithmetic: 21 us -> none  [attend(): probs_bf = jax.nn.softmax(scores, axis=-1).astype(jnp.bfloat16)]
    dot_general x10 -> x6, matrix products: 18.6 us -> 34.6 us  [the longest x1 20.5 us: local_layer(): jnp.dot(at_pos.astype(F32), bias_table(rel_bias, t_len), precision=lax.Pr...]
    convert_element_type x6 -> x3, other arithmetic: 5.48 us -> 0.78 us  [the longest x1 0.69 us: rms_norm(): return (values * inv_rms * norm_scale.astype(F32)).astype(BF16)]
    gather x2 -> x0, local copies, waits for them, and re-layouts: 3.92 us -> none  [self_terms(): jnp.take(rel_bias, rel_bucket(distance), axis=0)]
    slice x0 -> x2, local copies, waits for them, and re-layouts: none -> 3.9 us  [bias_table(): table = jnp.where(distance >= edge, rel_bias[bucket + 1, 0], table)]
    dot_general x1 -> x0, other arithmetic: 3.73 us -> none  [attend(): jnp.einsum('bhk,bthk->bht', queries, keys_all, preferred_element_type=jnp...]
  transfers between devices with their start and end apart: 3 -> 0, of which waited for: 3 -> 0; matrix products, arithmetic and copies ran while one was open for 0% -> 0% of each run, Pallas kernels for 0% -> 0%
where the time goes in v1:
time: 144 us; the launch traced here: 143 us
  Pallas kernels  81.5 us (57%)
  matrix products  34.6 us (24%)
  other arithmetic  15.1 us (10%)
  local copies, waits for them, and re-layouts  10.4 us (7%)
    pallas_call x1, Pallas kernels, tail(): pl.pallas_call(tail_kernel, out_shape=jax.ShapeDtypeStruct(x_in.shape, BF...  81.5 us
    dot_general x1, matrix products, local_layer(): jnp.dot(at_pos.astype(F32), bias_table(rel_bias, t_len), precision=lax.Pr...  20.5 us
    select_n x1, other arithmetic, local_layer(): new_self_v = jnp.where(at_pos[:, :, None, None], new_values, self_v)  12.6 us
    dot_general x1, matrix products, local_layer(): jnp.einsum('bht,bthk->bhk', probs, new_self_v, preferred_element_type=F32)  7.93 us
    unnamed x29, local copies, waits for them, and re-layouts  4.44 us
    dot_general x3, matrix products, project(): return jnp.dot(normed, weight, preferred_element_type=F32).astype(BF16)  3.97 us
    slice x2, local copies, waits for them, and re-layouts, bias_table(): table = jnp.where(distance >= edge, rel_bias[bucket + 1, 0], table)  3.9 us

profile of v1, /device:TPU:0, one launch (start us, length us, event | category | flops | bytes accessed | tf_op | source)
XLA Modules:
  0.0 142.7 jit_solution(3965798782977930328)
XLA Ops:
  0.6 0.0 copy-start
  0.6 0.0 copy-start.3
  0.7 0.0 copy-start.12
  0.7 0.0 copy-start.13
  0.7 1.6 %fusion.4 = f32[512]{0:T(512)S(1)} fusion(bf16[512,1024]{1,0:T(8,128)(2,1)} %x_hbm.1), kind=kLoop, calls=%fused_computation.8 | loop fusion | flops 1572352 | bytes 1050624 | tf_op jit(solution)/shard_map/reduce_sum | solution.py:18
  2.3 0.7 convert_element_type.28
  3.0 0.7 broadcast_in_dim.183.nc_ref
  3.7 0.7 broadcast_in_dim.184.nm_ref
  4.4 1.8 %fusion.203 = (f32[1,1]{0,1:T(1,128)}, f32[1,1]{0,1:T(1,128)}, f32[1,1]{0,1:T(1,128)}, f32[1,1]{0,1:T(1,128)}, f32[1,1]{0,1:T(1,128)}, /*index=5*/f32[1,1]{0,1:T...) fusion(f32[32,1]{0,1:T(1,128)} %param.27), kind=kLoop, calls=%fused_computation.183 | loop fusion | bytes 104 | tf_op jit(solution)/shard_map/slice | solution.py:269
  6.2 2.1 %fusion.202 = (f32[1,1]{0,1:T(1,128)}, f32[1,1]{0,1:T(1,128)}, f32[1,1]{0,1:T(1,128)}, f32[1,1]{0,1:T(1,128)}, f32[1,1]{0,1:T(1,128)}, /*index=5*/f32[1,1]{0,1:T...) fusion(f32[32,1]{0,1:T(1,128)} %param.27), kind=kLoop, calls=%fused_computation.182 | loop fusion | bytes 152 | tf_op jit(solution)/shard_map/slice | solution.py:269
  8.3 0.0 copy-done
  8.3 1.7 %convolution_convert_fusion.2 = bf16[512,64]{0,1:T(8,128)(2,1)S(1)} fusion(bf16[1024,64]{0,1:T(8,128)(2,1)S(1)} %copy-done, bf16[512,1024]{1,0:T(8,128)(2,1)} %x_hbm.1, f32[1024]{0:T(1024)S(1)} %convert_element_type.28, f32[512]{0:T(512)S(1)} %add_rsqrt_fusion), kind=kOutput, calls=%fused_computation.16 | convolution fusion | flops 69238784 | bytes 1251328 | tf_op jit(solution)/shard_map/dot_general | solution.py:23
  10.0 0.1 copy.24
  10.1 1.7 %convolution_convert_fusion.1 = bf16[512,64]{0,1:T(8,128)(2,1)S(1)} fusion(bf16[1024,64]{0,1:T(8,128)(2,1)} %param.30, bf16[512,1024]{1,0:T(8,128)(2,1)} %x_hbm.1, f32[1024]{0:T(1024)S(1)} %convert_element_type.28, f32[512]{0:T(512)S(1)} %add_rsqrt_fusion), kind=kOutput, calls=%fused_computation.15 | convolution fusion | flops 69238784 | bytes 1251328 | tf_op jit(solution)/shard_map/dot_general | solution.py:23
  11.9 0.1 copy.25
  12.0 0.0 copy-done.12
  12.1 0.2 copy.23
  12.2 0.0 copy-done.3
  12.3 0.0 copy-done.13
  12.3 0.5 fusion.8
  12.8 12.6 %broadcast_select_fusion = (bf16[512,128,1,64]{1,3,2,0:T(8,128)(2,1)}, bf16[512,128,1,64]{1,3,2,0:T(8,128)(2,1)S(1)}) fusion(bf16[512,128,1,64]{1,3,2,0:T(8,128)(2,1)} %param.23, pred[512,128]{1,0:T(8,128)(4,1)S(1)} %copy.23, bf16[512,64]{1,0:T(8,128)(2,1)S(1)} %copy.25, bf16[512,128,1,64]{1,3,2,0:T(8,128)(2,1)} %param.22, bf16[512,64]{1,0:T(8,128)(2,1)S(1)} %copy.24), kind=kLoop, calls=%fused_computation.4 | loop fusion | flops 8388608 | bytes 33751040 | tf_op jit(solution)/shard_map/jit(_where)/select_n | solution.py:285
  25.4 0.0 copy-start.11
  25.4 3.4 %copy-done.11 = bf16[512,128,1,64]{1,3,2,0:T(8,128)(2,1)} copy-done((bf16[512,128,1,64]{1,3,2,0:T(8,128)(2,1)}, bf16[512,128,1,64]{1,3,2,0:T(8,128)(2,1)S(1)}, u32[]{:S(2)}) %copy-start.11) | copy-done | bytes 8388632
  28.8 2.3 %fusion.2 = f32[512,1,128]{2,1,0:T(1,128)S(1)} fusion(bf16[512,128,1,64]{1,3,2,0:T(8,128)(2,1)S(1)} %get-tuple-element.43, bf16[512,64,1]{1,0,2:T(8,128)(2,1)S(1)} %fusion.8), kind=kOutput, calls=%fused_computation.2 | convolution fusion | flops 8388608 | bytes 8716288 | tf_op jit(solution)/shard_map/bhk,bthk->bht/dot_general | solution.py:286
  31.1 0.1 copy.27
  31.2 20.5 %fusion.204 = (f32[512]{0:T(512)S(1)}, f32[512,128]{0,1:T(8,128)S(1)}) fusion(f32[]{:T(128)} %bitcast.34, f32[]{:T(128)} %bitcast.33, f32[]{:T(128)} %bitcast.32, f32[]{:T(128)} %bitcast.31, f32[]{:T(128)} %bitcast.30, f32[]{:T(128)} %bitcast.29, f32[]{:T(128)} %bitcast.28, f32[]{:T(128)} %bitcast.27, f32[]{:T(128)} %bitcast.26, f32[]{:T(128)} %bitcast.25, ...), kind=kOutput, calls=%fused_computation.184 | convolution fusion | flops 102022656 | bytes 528512 | tf_op jit(solution)/shard_map/dot_general | solution.py:282
  51.7 0.1 fusion.10
  51.7 0.0 copy-start.6
  51.7 0.0 copy-start.8
  51.8 0.0 copy-start.9
  51.8 0.0 copy-start.10
  51.8 0.1 fusion.11
  51.8 0.2 copy.28
  52.0 0.0 copy-start.1
  52.0 0.0 copy-start.2
  52.0 0.0 copy-start.4
  52.0 0.0 copy-start.5
  52.1 0.0 copy-start.7
  52.1 7.9 %fusion = f32[512,1,64]{2,1,0:T(1,128)S(1)} fusion(bf16[512,128,1]{1,2,0:T(2,128)(2,1)S(1)} %copy.28, bf16[512,128,1,64]{1,3,2,0:T(8,128)(2,1)} %get-tuple-element.44), kind=kOutput, calls=%fused_computation | convolution fusion | flops 8388608 | bytes 8650752 | tf_op jit(solution)/shard_map/bht,bthk->bhk/dot_general | solution.py:288
  60.0 0.0 copy-done.6
  60.1 0.0 copy-done.8
  60.1 0.0 copy-done.9
  60.1 0.0 copy-done.10
  60.1 0.0 copy-done.1
  60.1 0.0 copy-done.2
  60.1 0.0 copy-done.4
  60.1 0.0 copy-done.5
  60.1 0.0 copy-done.7
  60.1 81.5 %tail.1 = bf16[512,1024]{1,0:T(8,128)(2,1)S(1)} custom-call(bf16[512,1024]{1,0:T(8,128)(2,1)S(1)} %copy-done.3, bf16[512,64]{1,0:T(8,128)(2,1)S(1)} %convert_element_type.34.attn_ref, s32[64,512]{1,0:T(8,128)S(1)} %bitcast.64, bf16[64,64,512]{2,1,0:T(8,128)(2,1)S(1)} %bitcast.60, bf16[64,64,512]{2,1,0:T(8,128)(2,1)S(1)} %bitcast.61, ...), custom_call_target="tpu_custom_call" | custom-call | tf_op jit(solution)/shard_map/tail/pallas_call | solution.py:254
  141.7 1.0 copy.33
  (3 shorter events, 0.1 us)
Async XLA Ops:
  0.6 7.6 %copy-start = (bf16[1024,64]{0,1:T(8,128)(2,1)S(1)}, bf16[1024,64]{0,1:T(8,128)(2,1)}, u32[]{:S(2)}) copy-start(bf16[1024,64]{0,1:T(8,128)(2,1)} %param.29) | copy-start | bytes 393220
  0.6 11.6 %copy-start.3 = (bf16[512,1024]{1,0:T(8,128)(2,1)S(1)}, bf16[512,1024]{1,0:T(8,128)(2,1)}, u32[]{:S(2)}) copy-start(bf16[512,1024]{1,0:T(8,128)(2,1)} %x_hbm.1) | copy-start | bytes 3145732
  0.7 11.4 %copy-start.12 = (s32[512]{0:T(512)S(1)}, s32[512]{0:T(512)}, u32[]{:S(2)}) copy-start(s32[512]{0:T(512)} %param.21) | copy-start | bytes 6148
  0.7 11.6 %copy-start.13 = (bf16[1024,64]{0,1:T(8,128)(2,1)S(1)}, bf16[1024,64]{0,1:T(8,128)(2,1)}, u32[]{:S(2)}) copy-start(bf16[1024,64]{0,1:T(8,128)(2,1)} %param.28) | copy-start | bytes 393220
  25.4 3.4 %copy-start.11 = (bf16[512,128,1,64]{1,3,2,0:T(8,128)(2,1)}, bf16[512,128,1,64]{1,3,2,0:T(8,128)(2,1)S(1)}, u32[]{:S(2)}) copy-start(bf16[512,128,1,64]{1,3,2,0:T(8,128)(2,1)S(1)} %get-tuple-element.43) | copy-start | bytes 25165828
  51.7 8.3 %copy-start.6 = (bf16[176,1024]{1,0:T(8,128)(2,1)S(1)}, bf16[176,1024]{1,0:T(8,128)(2,1)}, u32[]{:S(2)}) copy-start(bf16[176,1024]{1,0:T(8,128)(2,1)} %wd_hbm.1) | copy-start | bytes 1081348
  51.7 8.3 %copy-start.8 = (bf16[64,1024]{1,0:T(8,128)(2,1)S(1)}, bf16[64,1024]{1,0:T(8,128)(2,1)}, u32[]{:S(2)}) copy-start(bf16[64,1024]{1,0:T(8,128)(2,1)} %wo_hbm.1) | copy-start | bytes 393220
  51.8 8.3 %copy-start.9 = (bf16[1024,64]{0,1:T(8,128)(2,1)S(1)}, bf16[1024,64]{0,1:T(8,128)(2,1)}, u32[]{:S(2)}) copy-start(bf16[1024,64]{0,1:T(8,128)(2,1)} %param.32) | copy-start | bytes 393220
  51.8 8.3 %copy-start.10 = (bf16[64,1024]{1,0:T(8,128)(2,1)S(1)}, bf16[64,1024]{1,0:T(8,128)(2,1)}, u32[]{:S(2)}) copy-start(bf16[64,1024]{1,0:T(8,128)(2,1)} %co_hbm.1) | copy-start | bytes 393220
  52.0 8.1 %copy-start.1 = (bf16[512,64,1,64]{0,3,2,1:T(8,128)(2,1)S(1)}, bf16[512,64,1,64]{0,3,2,1:T(8,128)(2,1)}, u32[]{:S(2)}) copy-start(bf16[512,64,1,64]{0,3,2,1:T(8,128)(2,1)} %param.24) | copy-start | bytes 12582916
  52.0 8.1 %copy-start.2 = (bf16[512,64,1,64]{0,3,2,1:T(8,128)(2,1)S(1)}, bf16[512,64,1,64]{0,3,2,1:T(8,128)(2,1)}, u32[]{:S(2)}) copy-start(bf16[512,64,1,64]{0,3,2,1:T(8,128)(2,1)} %param.25) | copy-start | bytes 12582916
  52.0 8.1 %copy-start.4 = (bf16[1024,176]{0,1:T(8,128)(2,1)S(1)}, bf16[1024,176]{0,1:T(8,128)(2,1)}, u32[]{:S(2)}) copy-start(bf16[1024,176]{0,1:T(8,128)(2,1)} %param.34) | copy-start | bytes 1081348
  52.0 8.1 %copy-start.5 = (bf16[1024,176]{0,1:T(8,128)(2,1)S(1)}, bf16[1024,176]{0,1:T(8,128)(2,1)}, u32[]{:S(2)}) copy-start(bf16[1024,176]{0,1:T(8,128)(2,1)} %param.35) | copy-start | bytes 1081348
  52.1 8.1 %copy-start.7 = (s32[512,64]{0,1:T(8,128)S(1)}, s32[512,64]{0,1:T(8,128)}, u32[]{:S(2)}) copy-start(s32[512,64]{0,1:T(8,128)} %param.26) | copy-start | bytes 393220

commit v2 on v1

--- a/solution.py
+++ b/solution.py
@@ -17,10 +17,6 @@
 def rms_norm(values, norm_scale):
     inv_rms = lax.rsqrt(jnp.mean(values * values, axis=-1, keepdims=True) + 1e-6)
     return (values * inv_rms * norm_scale.astype(F32)).astype(BF16)
-
-
-def project(normed, weight):
-    return jnp.dot(normed, weight, preferred_element_type=F32).astype(BF16)
 
 
 def gelu_tanh(u):
@@ -235,7 +231,7 @@
 
 
 def tail(x_in, attn, mask_t, ck_t, cv_t, wo, cq_t, co, wg_t, wu_t, wd, nc, nm):
-    any_spec = pl.BlockSpec(memory_space=pl.ANY)
+    hbm = pl.BlockSpec(memory_space=pltpu.HBM)
     vmem = pl.BlockSpec(memory_space=pltpu.VMEM)
     units = wd.shape[0]
     dma = pltpu.SemaphoreType.DMA
@@ -254,39 +250,125 @@
     return pl.pallas_call(
         tail_kernel,
         out_shape=jax.ShapeDtypeStruct(x_in.shape, BF16),
-        in_specs=[any_spec, vmem, vmem] + [any_spec] * 8 + [vmem, vmem],
+        in_specs=[hbm, vmem, vmem] + [hbm] * 8 + [vmem, vmem],
         out_specs=vmem,
         scratch_shapes=scratch,
-        compiler_params=pltpu.CompilerParams(collective_id=0, has_side_effects=True, vmem_limit_bytes=40 * 1024 * 1024),
+        compiler_params=pltpu.CompilerParams(collective_id=0, has_side_effects=True, vmem_limit_bytes=60 * 1024 * 1024),
         name="tail",
     )(x_in, attn, mask_t, ck_t, cv_t, wo, cq_t, co, wg_t, wu_t, wd, nc, nm)
 
 
-def bias_table(rel_bias, t_len):
-    distance = jnp.arange(t_len)[:, None] - jnp.arange(t_len)[None, :]
-    table = jnp.full((t_len, t_len), rel_bias[0, 0], F32)
+def head_kernel(tok_ref, rb_ref, x_ref, wq_ref, wk_ref, wv_ref, ns_ref, k_hbm, v_hbm,
+                attn_ref, nk_hbm, nv_hbm,
+                kbuf, vbuf, h_buf, qq, k_new, v_new, table, in_sem, out_sem):
+    rows, depth, t_len = kbuf.shape
+    n_chunks = in_sem.shape[1]
+    size = rows // n_chunks
+
+    def chunk_copy(i, which):
+        hbm, buf = ((k_hbm, kbuf), (v_hbm, vbuf))[which]
+        part = pl.ds(i * size, size)
+        return pltpu.make_async_copy(hbm.at[part], buf.at[part], in_sem.at[which, i])
+
+    def chunk_out(i, which):
+        hbm, buf = ((nk_hbm, kbuf), (nv_hbm, vbuf))[which]
+        part = pl.ds(i * size, size)
+        return pltpu.make_async_copy(buf.at[part], hbm.at[part], out_sem.at[which, i])
+
+    for i in range(n_chunks):
+        chunk_copy(i, 0).start()
+        chunk_copy(i, 1).start()
+
+    distance = lax.broadcasted_iota(jnp.int32, (t_len, t_len), 0) - lax.broadcasted_iota(jnp.int32, (t_len, t_len), 1)
+    bias = jnp.full((t_len, t_len), rb_ref[0], F32)
     for bucket, edge in enumerate(BUCKET_EDGES):
-        table = jnp.where(distance >= edge, rel_bias[bucket + 1, 0], table)
-    return table
+        bias = jnp.where(distance >= edge, rb_ref[bucket + 1], bias)
+    table[...] = jnp.where(distance >= 0, bias, NEG_FILL)
+
+    wqq = jnp.concatenate([wq_ref[...], wq_ref[...]], axis=0)
+    for i in range(rows // 128):
+        part = slice(i * 128, i * 128 + 128)
+        h = rms_norm(x_ref[part, :].astype(F32), ns_ref[...])
+        qq[part, :] = dot_nt(h, wqq).astype(BF16).astype(F32)
+        k_new[i] = dot_nt(wk_ref[...], h).astype(BF16).astype(F32)
+        v_new[i] = dot_nt(wv_ref[...], h).astype(BF16).astype(F32)
+
+    lane = lax.broadcasted_iota(jnp.int32, (depth, t_len), 1)
+    row8 = lax.broadcasted_iota(jnp.int32, (8, 128), 0)
+    half8 = lax.broadcasted_iota(jnp.int32, (8, 128), 1) // depth
+
+    def step(i, carry):
+        chunk_copy(i, 0).wait()
+        chunk_copy(i, 1).wait()
+        shift = lax.rem(i, 2) * size
+        k_cols = pltpu.roll(k_new[i // 2], shift, 1)
+        v_cols = pltpu.roll(v_new[i // 2], shift, 1)
+        scores = []
+        for g in range(size // 8):
+            k8, bias8 = [], []
+            for j in range(8):
+                b = i * size + g * 8 + j
+                pos = tok_ref[b]
+                at_pos = lane == pos
+                col = g * 8 + j
+                k_b = jnp.where(at_pos, jnp.broadcast_to(k_cols[:, col:col + 1], (depth, t_len)), kbuf[b].astype(F32)).astype(BF16)
+                v_b = jnp.where(at_pos, jnp.broadcast_to(v_cols[:, col:col + 1], (depth, t_len)), vbuf[b].astype(F32)).astype(BF16)
+                kbuf[b] = k_b
+                vbuf[b] = v_b
+                k8.append(k_b)
+                bias8.append(table[pl.ds(pos, 1), :])
+            q8 = qq[pl.ds(pl.multiple_of(i * size + g * 8, 8), 8), :]
+            q_diag = jnp.concatenate([jnp.where(row8 == 2 * m + half8, q8, 0.0) for m in range(4)], axis=1).astype(BF16)
+            scores.append(dot_nn(q_diag, jnp.concatenate(k8, axis=0)) + jnp.concatenate(bias8, axis=0))
+        chunk_out(i, 0).start()
+        chunk_out(i, 1).start()
+        s = jnp.concatenate(scores, axis=0)
+        e = jnp.exp(s - jnp.max(s, axis=1, keepdims=True))
+        p = (e / jnp.sum(e, axis=1, keepdims=True)).astype(BF16).astype(F32)
+        outs = []
+        for g in range(size // 8):
+            p8 = p[g * 8:g * 8 + 8, :]
+            p_diag = jnp.concatenate([jnp.where(row8 == j, p8, 0.0) for j in range(8)], axis=1).astype(BF16)
+            v8 = jnp.concatenate([vbuf[i * size + g * 8 + j] for j in range(8)], axis=1)
+            outs.append(dot_nt(p_diag, v8))
+        attn_ref[pl.ds(pl.multiple_of(i * size, size), size), :] = jnp.concatenate(outs, axis=0).astype(BF16)
+        return carry
+
+    lax.fori_loop(0, n_chunks, step, 0)
+    for i in range(n_chunks):
+        chunk_out(i, 0).wait()
+        chunk_out(i, 1).wait()
+
+
+def head(tok_pos, rel_bias, x_in, wq_t, wk_t, wv_t, ns, k_t, v_t):
+    hbm = pl.BlockSpec(memory_space=pltpu.HBM)
+    vmem = pl.BlockSpec(memory_space=pltpu.VMEM)
+    smem = pl.BlockSpec(memory_space=pltpu.SMEM)
+    rows, depth, t_len = k_t.shape
+    dma = pltpu.SemaphoreType.DMA
+    n_chunks = 8
+    return pl.pallas_call(
+        head_kernel,
+        out_shape=(jax.ShapeDtypeStruct((rows, depth), BF16), jax.ShapeDtypeStruct(k_t.shape, BF16), jax.ShapeDtypeStruct(v_t.shape, BF16)),
+        in_specs=[smem, smem] + [vmem] * 5 + [hbm] * 2,
+        out_specs=(vmem, hbm, hbm),
+        scratch_shapes=[
+            pltpu.VMEM(k_t.shape, BF16), pltpu.VMEM(v_t.shape, BF16), pltpu.VMEM((8, 128), BF16),
+            pltpu.VMEM((rows, 2 * depth), F32), pltpu.VMEM((rows // 128, depth, 128), F32), pltpu.VMEM((rows // 128, depth, 128), F32),
+            pltpu.VMEM((t_len, t_len), F32), dma((2, n_chunks)), dma((2, n_chunks)),
+        ],
+        compiler_params=pltpu.CompilerParams(vmem_limit_bytes=60 * 1024 * 1024),
+        name="head",
+    )(tok_pos, rel_bias, x_in, wq_t, wk_t, wv_t, ns, k_t, v_t)
 
 
 def solution(mesh):
     def local_layer(x_in, tok_pos, self_k, self_v, cross_k, cross_v, enc_mask, rel_bias, w_q, w_k, w_v, w_o, cross_q, cross_o, w_gate, w_up, w_down, norm_self, norm_cross, norm_mlp):
-        row_count, t_len, _, head_dim = self_k.shape
-        normed = rms_norm(x_in.astype(F32), norm_self)
-        queries = project(normed, w_q)[:, None, :]
-        new_keys = project(normed, w_k)[:, None, None, :]
-        new_values = project(normed, w_v)[:, None, None, :]
-        key_index = jnp.arange(t_len)
-        at_pos = key_index[None, :] == tok_pos[:, None]
-        bias = jnp.dot(at_pos.astype(F32), bias_table(rel_bias, t_len), precision=lax.Precision.HIGHEST)
-        extra = jnp.where(key_index[None, :] <= tok_pos[:, None], bias, NEG_FILL)[:, None, :]
-        new_self_k = jnp.where(at_pos[:, :, None, None], new_keys, self_k)
-        new_self_v = jnp.where(at_pos[:, :, None, None], new_values, self_v)
-        scores = jnp.einsum('bhk,bthk->bht', queries, new_self_k, preferred_element_type=F32) + extra
-        probs = jax.nn.softmax(scores, axis=-1).astype(BF16)
-        mixed = jnp.einsum('bht,bthk->bhk', probs, new_self_v, preferred_element_type=F32).astype(BF16)
-        attn = mixed.reshape(row_count, head_dim)
+        k_t = jnp.transpose(self_k[:, :, 0, :], (0, 2, 1))
+        v_t = jnp.transpose(self_v[:, :, 0, :], (0, 2, 1))
+        attn, new_k, new_v = head(tok_pos, rel_bias[:, 0], x_in, w_q.T, w_k.T, w_v.T, norm_self[None, :], k_t, v_t)
+        new_self_k = jnp.transpose(new_k, (0, 2, 1))[:, :, None, :]
+        new_self_v = jnp.transpose(new_v, (0, 2, 1))[:, :, None, :]
         ck_t = jnp.transpose(cross_k[:, :, 0, :], (1, 2, 0))
         cv_t = jnp.transpose(cross_v[:, :, 0, :], (1, 2, 0))
         out = tail(x_in, attn, enc_mask.T, ck_t, cv_t, w_o, cross_q.T, cross_o, w_gate.T, w_up.T, w_down,

time: 144 us -> 104 us (0.72)
  matrix products: 34.6 us -> 0 us
  Pallas kernels: 81.5 us -> 97 us
  other arithmetic: 15.1 us -> 0 us
  local copies, waits for them, and re-layouts: 10.4 us -> 6.08 us
    dot_general x6 -> x0, matrix products: 34.6 us -> none  [the longest x1 20.5 us: local_layer(): jnp.dot(at_pos.astype(F32), bias_table(rel_bias, t_len), precision=lax.Pr...]
    pallas_call x0 -> x1, Pallas kernels: none -> 15.2 us  [head(): pl.pallas_call(head_kernel, out_shape=(jax.ShapeDtypeStruct((rows, depth)...]
    select_n x1 -> x0, other arithmetic: 12.6 us -> none  [local_layer(): new_self_v = jnp.where(at_pos[:, :, None, None], new_values, self_v)]
    slice x2 -> x0, local copies, waits for them, and re-layouts: 3.9 us -> none  [bias_table(): table = jnp.where(distance >= edge, rel_bias[bucket + 1, 0], table)]
    unnamed x29 -> x1, local copies, waits for them, and re-layouts: 4.44 us -> 2.26 us
    reduce_sum x2 -> x0, other arithmetic: 1.67 us -> none  [the longest x1 1.6 us: rms_norm(): jnp.mean(values * values, axis=-1, keepdims=True) + 1e-06]
where the time goes in v2:
time: 104 us
  Pallas kernels  97 us (93%)
  local copies, waits for them, and re-layouts  6.08 us (6%)
    pallas_call x1, Pallas kernels, tail(): pl.pallas_call(tail_kernel, out_shape=jax.ShapeDtypeStruct(x_in.shape, BF...  81.8 us
    pallas_call x1, Pallas kernels, head(): pl.pallas_call(head_kernel, out_shape=(jax.ShapeDtypeStruct((rows, depth)...  15.2 us
    unnamed x1, local copies, waits for them, and re-layouts  2.26 us

profile of v2, /device:TPU:0, one launch (start us, length us, event | category | flops | bytes accessed | tf_op | source)
XLA Modules:
  0.0 103.8 jit_solution(9883622030163796581)
XLA Ops:
  0.6 1.3 %broadcast_in_dim.15.ns_ref = bf16[1,1024]{1,0:T(2,128)(2,1)} reshape(bf16[1024]{0:T(1024)(128)(2,1)} %param.37) | data formatting | bytes 4096 | tf_op jit(solution)/shard_map/broadcast_in_dim | solution.py:369
  1.9 1.3 %broadcast_in_dim.16.nc_ref = bf16[1,1024]{1,0:T(2,128)(2,1)} reshape(bf16[1024]{0:T(1024)(128)(2,1)} %param.38) | data formatting | bytes 4096 | tf_op jit(solution)/shard_map/broadcast_in_dim | solution.py:375
  3.2 1.3 %broadcast_in_dim.17.nm_ref = bf16[1,1024]{1,0:T(2,128)(2,1)} reshape(bf16[1024]{0:T(1024)(128)(2,1)} %param.39) | data formatting | bytes 4096 | tf_op jit(solution)/shard_map/broadcast_in_dim | solution.py:375
  4.4 15.2 %head.1 = (bf16[512,64]{1,0:T(8,128)(2,1)}, bf16[512,64,128]{2,1,0:T(8,128)(2,1)}, bf16[512,64,128]{2,1,0:T(8,128)(2,1)}) custom-call(s32[512]{0:T(512)} %tok_ref.1, f32[32]{0:T(128)} %bitcast.41, bf16[512,1024]{1,0:T(8,128)(2,1)} %x_hbm.1, bf16[64,1024]{1,0:T(8,128)(2,1)} %bitcast.36, bf16[64,1024]{1,0:T(8,128)(2,1)} %bitcast.37, ...), custom_call_target="tpu_custom_call" | custom-call | tf_op jit(solution)/shard_map/head/pallas_call | solution.py:350
  19.7 81.8 %tail.1 = bf16[512,1024]{1,0:T(8,128)(2,1)} custom-call(bf16[512,1024]{1,0:T(8,128)(2,1)} %x_hbm.1, bf16[512,64]{1,0:T(8,128)(2,1)} %get-tuple-element.6.attn_ref, s32[64,512]{1,0:T(8,128)} %bitcast.39, bf16[64,64,512]{2,1,0:T(8,128)(2,1)} %bitcast.32, bf16[64,64,512]{2,1,0:T(8,128)(2,1)} %bitcast.33, bf16[64,1024]{1,0:T(8,128)(2,1)} %wo_hbm.1, ...), custom_call_target="tpu_custom_call" | custom-call | tf_op jit(solution)/shard_map/tail/pallas_call | solution.py:250
  101.5 2.3 %copy.26 = bf16[512,1024]{1,0:T(8,128)(2,1)} copy(bf16[512,1024]{1,0:T(8,128)(2,1)} %tail.1) | data formatting | bytes 2097152

commit v3 on v2

v3 whole, which is shorter than its diff:
```python
import math
import jax
import jax.numpy as jnp
from jax import lax
from jax.experimental import pallas as pl
from jax.experimental.pallas import tpu as pltpu
from jax.sharding import PartitionSpec as P

BUCKET_EDGES = tuple(range(1, 16)) + (16,) + tuple(int(math.ceil(16.0 * 8.0 ** (m / 16.0))) for m in range(1, 16))
NEG_FILL = -1e30
MESH = pl.DeviceIdType.MESH
F32 = jnp.float32
BF16 = jnp.bfloat16
K_ORDER = (2, 1, 3)


def rms_norm(values, norm_scale):
    inv_rms = lax.rsqrt(jnp.mean(values * values, axis=-1, keepdims=True) + 1e-6)
    return (values * inv_rms * norm_scale.astype(F32)[None, :]).astype(BF16)


def gelu_tanh(u):
    return u * (0.5 * (1.0 + jnp.tanh(math.sqrt(2.0 / math.pi) * (u + 0.044715 * (u * u * u)))))


def dot_nt(a, b):
    return lax.dot_general(a, b, (((1,), (1,)), ((), ())), preferred_element_type=F32)


def dot_nn(a, b):
    return jnp.dot(a, b, preferred_element_type=F32)


def tail_kernel(x_hbm, attn_ref, mask_ref, ck_hbm, cv_hbm, wo_hbm, cq_hbm, co_hbm, wg_hbm, wu_hbm, wd_hbm, nc_ref, nm_ref,
                out_ref,
                x_buf, ck, cv, wo2, cq2, co2, wg2, wu2, wd2, att_in, pair, q_snd, q_all, o_snd, o_rcv, scores,
                y_snd, y_rcv, own, z_snd, z_rcv, h_buf, act,
                loc_sem, w_ssem, w_rsem, ys_sem, yr_sem, zs_sem, zr_sem, gys_sem, gyr_sem, gzs_sem, gzr_sem, cs_sem, cr_sem):
    me = lax.axis_index("tp")
    c = lax.rem(me, 2)
    y = lax.rem(me // 2, 2)
    z = me // 4
    core_peer = {"tp": z * 4 + y * 2 + (1 - c)}
    y_peer = {"tp": z * 4 + (1 - y) * 2 + c}
    z_peer = {k: {"tp": lax.rem(z + k, 4) * 4 + y * 2 + c} for k in (1, 2, 3)}
    sends = []

    def remote(src, dst, ssem, rsem, peer):
        return pltpu.make_async_remote_copy(src_ref=src, dst_ref=dst, send_sem=ssem, recv_sem=rsem, device_id=peer, device_id_type=MESH)

    def start(src, dst, ssem, rsem, peer):
        copy = remote(src, dst, ssem, rsem, peer)
        copy.start()
        sends.append(copy)
        return copy

    def span(base, size):
        return pl.ds(pl.multiple_of(base, size), size)

    def chunk(base, zz):
        return span(base + zz * 16, 16)

    half = wg2.shape[0] // 2
    local = [
        pltpu.make_async_copy(x_hbm.at[chunk(c * 256 + y * 64, z)], x_buf.at[0], loc_sem.at[0]),
        pltpu.make_async_copy(x_hbm.at[chunk(c * 256 + 128 + y * 64, z)], x_buf.at[1], loc_sem.at[1]),
        pltpu.make_async_copy(wo_hbm, wo2.at[pl.ds(0, 64)], loc_sem.at[2]),
        pltpu.make_async_copy(cq_hbm, cq2.at[0], loc_sem.at[3]),
        pltpu.make_async_copy(ck_hbm, ck, loc_sem.at[4]),
        pltpu.make_async_copy(cv_hbm, cv, loc_sem.at[5]),
        pltpu.make_async_copy(co_hbm, co2.at[pl.ds(0, 64)], loc_sem.at[6]),
        pltpu.make_async_copy(wg_hbm, wg2.at[pl.ds(0, half)], loc_sem.at[7]),
        pltpu.make_async_copy(wu_hbm, wu2.at[pl.ds(0, half)], loc_sem.at[8]),
        pltpu.make_async_copy(wd_hbm, wd2.at[pl.ds(0, half)], loc_sem.at[9]),
    ]
    for copy in local:
        copy.start()

    barrier = pltpu.get_barrier_semaphore()
    for peer in (core_peer, y_peer, z_peer[1], z_peer[2], z_peer[3]):
        pl.semaphore_signal(barrier, inc=1, device_id=peer, device_id_type=MESH)
    pl.semaphore_wait(barrier, 5)

    att_copy = start(attn_ref.at[span((1 - c) * 256, 256)], att_in, w_ssem.at[0], w_rsem.at[0], core_peer)
    wo_copy = start(wo_hbm, wo2.at[pl.ds(64, 64)], w_ssem.at[1], w_rsem.at[1], core_peer)
    cq_copy = start(cq_hbm, cq2.at[1], w_ssem.at[2], w_rsem.at[2], core_peer)
    co_copy = start(co_hbm, co2.at[pl.ds(64, 64)], w_ssem.at[3], w_rsem.at[3], core_peer)
    wg_copy = start(wg_hbm, wg2.at[pl.ds(half, half)], w_ssem.at[4], w_rsem.at[4], core_peer)
    wu_copy = start(wu_hbm, wu2.at[pl.ds(half, half)], w_ssem.at[5], w_rsem.at[5], core_peer)
    wd_copy = start(wd_hbm, wd2.at[pl.ds(half, half)], w_ssem.at[6], w_rsem.at[6], core_peer)
    waited = set()

    def once(name, *waits):
        if name not in waited:
            waited.add(name)
            for wait in waits:
                wait()

    def reduce_scatter(p, b, partial_of):
        y_snd[p, b] = partial_of((1 - y) * 64).astype(BF16)
        y_copies = {}
        for k in K_ORDER + (0,):
            y_copies[k] = start(y_snd.at[p, b, chunk(0, lax.rem(z + k, 4))], y_rcv.at[p, b, k], ys_sem.at[p, b, k], yr_sem.at[p, b, k], y_peer)
        own[b] = partial_of(y * 64)
        yield
        z_copies = {}
        for k in K_ORDER:
            y_copies[k].wait_recv()
            z_snd[p, b, k - 1] = (own[b, chunk(0, lax.rem(z + k, 4))] + y_rcv[p, b, k].astype(F32)).astype(BF16)
            z_copies[k] = start(z_snd.at[p, b, k - 1], z_rcv.at[p, b, k - 1], zs_sem.at[p, b, k - 1], zr_sem.at[p, b, k - 1], z_peer[k])
        yield
        y_copies[0].wait_recv()
        total = own[b, chunk(0, z)] + y_rcv[p, b, 0].astype(F32)
        for k in (1, 3, 2):
            z_copies[k].wait_recv()
            total = total + z_rcv[p, b, k - 1].astype(F32)
        return total

    def gather(p, b, buf, base, on_part=None):
        def part_at(yy, k):
            return buf.at[chunk(base + yy * 64, lax.rem(z + 4 - k, 4))]

        def done(part, slot):
            if on_part is not None:
                on_part(part, slot)

        mine = part_at(y, 0)
        start(mine, mine, gys_sem.at[p, b, 0], gyr_sem.at[p, b, 0], y_peer)
        for k in K_ORDER:
            start(mine, mine, gzs_sem.at[p, b, k - 1], gzr_sem.at[p, b, k - 1], z_peer[k])
        done(mine, 0)
        yield
        for k in (1, 3, 2):
            part = part_at(y, k)
            remote(part, part, gzs_sem.at[p, b, k - 1], gzr_sem.at[p, b, k - 1], z_peer[k]).wait_recv()
            start(part, part, gys_sem.at[p, b, k], gyr_sem.at[p, b, k], y_peer)
            done(part, k)
        yield
        for k in (0, 1, 3, 2):
            part = part_at(1 - y, k)
            remote(part, part, gys_sem.at[p, b, k], gyr_sem.at[p, b, k], y_peer).wait_recv()
            done(part, 4 + k)

    def cross(half_id, b):
        lanes = span(half_id * 256 + b * 128, 128)
        q_blk = q_all[half_id, b].astype(F32)

        def score_step(i, carry):
            rows = span(i * 8, 8)
            scores[rows, :] = jnp.sum(ck[rows, :, lanes].astype(F32) * q_blk[None], axis=1)
            return carry

        lax.fori_loop(0, 8, score_step, 0)
        s = scores[...] + jnp.where(mask_ref[:, lanes] != 0, 0.0, NEG_FILL)
        e = jnp.exp(s - jnp.max(s, axis=0, keepdims=True))
        scores[...] = (e / jnp.sum(e, axis=0, keepdims=True)).astype(BF16).astype(F32)

        def mix_step(i, acc):
            p_blk = scores[span(i * 8, 8), :]
            for j in range(8):
                acc = acc + cv[i * 8 + j, :, lanes].astype(F32) * p_blk[j:j + 1, :]
            return acc

        return lax.fori_loop(0, 8, mix_step, jnp.zeros((64, 128), F32)).astype(BF16)

    def flow(b):
        once("att", att_copy.wait_recv, local[2].wait, wo_copy.wait_recv)
        pair[b, :, 0:64] = attn_ref[span(c * 256 + b * 128, 128), :]
        pair[b, :, 64:128] = att_in[b * 128:b * 128 + 128, :]
        total = yield from reduce_scatter(0, b, lambda base: dot_nn(pair[b, span(base, 64)], wo2[...]))
        local[b].wait()
        resid = x_buf[b].astype(F32) + total
        h_buf[0, b, chunk(y * 64, z)] = rms_norm(resid, nc_ref[...])
        yield from gather(0, b, h_buf.at[0, b], 0)
        once("cq", cq_copy.wait_recv, local[3].wait, local[4].wait, local[5].wait)
        q_snd[b] = dot_nt(cq2[1], h_buf[0, b]).astype(BF16)
        q_copy = start(q_snd.at[b], q_all.at[c, b], w_ssem.at[7 + b], w_rsem.at[7 + b], core_peer)
        q_all[c, b] = dot_nt(cq2[0], h_buf[0, b]).astype(BF16)
        mine = cross(c, b)
        pair[b, :, 0:64] = mine.astype(F32).T.astype(BF16)
        remote(q_snd.at[b], q_all.at[1 - c, b], w_ssem.at[7 + b], w_rsem.at[7 + b], core_peer).wait_recv()
        o_snd[b] = cross(1 - c, b)
        o_copy = start(o_snd.at[b], o_rcv.at[b], w_ssem.at[9 + b], w_rsem.at[9 + b], core_peer)
        yield
        o_copy.wait_recv()
        pair[b, :, 64:128] = o_rcv[b].astype(F32).T.astype(BF16)
        once("co", local[6].wait, co_copy.wait_recv)
        total = yield from reduce_scatter(1, b, lambda base: dot_nn(pair[b, span(base, 64)], co2[...]))
        resid = resid + total
        h_buf[1, b, chunk(y * 64, z)] = rms_norm(resid, nm_ref[...])
        yield from gather(1, b, h_buf.at[1, b], 0)
        once("mlp", local[7].wait, local[8].wait, local[9].wait, wg_copy.wait_recv, wu_copy.wait_recv, wd_copy.wait_recv)
        h = h_buf[1, b]
        act[b] = (gelu_tanh(dot_nt(h, wg2[...])) * dot_nt(h, wu2[...])).astype(BF16)
        total = yield from reduce_scatter(2, b, lambda base: dot_nn(act[b, span(base, 64)], wd2[...]))
        resid = resid + total
        first = c * 256 + b * 128
        out_ref[chunk(first + y * 64, z)] = resid.astype(BF16)
        yield from gather(2, b, out_ref, first, lambda part, slot: start(part, part, cs_sem.at[b, slot], cr_sem.at[b, slot], core_peer))

    flows = [flow(0), flow(1)]
    while flows:
        for item in list(flows):
            try:
                next(item)
            except StopIteration:
                flows.remove(item)
    for b in range(2):
        for slot in range(8):
            yy = y if slot < 4 else 1 - y
            part = out_ref.at[chunk((1 - c) * 256 + b * 128 + yy * 64, lax.rem(z + 4 - slot % 4, 4))]
            remote(part, part, cs_sem.at[b, slot], cr_sem.at[b, slot], core_peer).wait_recv()
    for copy in sends:
        copy.wait_send()


def tail(x_in, attn, mask_t, ck_t, cv_t, wo, cq_t, co, wg_t, wu_t, wd, nc, nm):
    hbm = pl.BlockSpec(memory_space=pltpu.HBM)
    vmem = pl.BlockSpec(memory_space=pltpu.VMEM)
    units = wd.shape[0]
    dma = pltpu.SemaphoreType.DMA
    scratch = [
        pltpu.VMEM((2, 16, 1024), BF16), pltpu.VMEM(ck_t.shape, BF16), pltpu.VMEM(cv_t.shape, BF16),
        pltpu.VMEM((128, 1024), BF16), pltpu.VMEM((2, 64, 1024), BF16), pltpu.VMEM((128, 1024), BF16),
        pltpu.VMEM((2 * units, 1024), BF16), pltpu.VMEM((2 * units, 1024), BF16), pltpu.VMEM((2 * units, 1024), BF16),
        pltpu.VMEM((256, 64), BF16), pltpu.VMEM((2, 128, 128), BF16), pltpu.VMEM((2, 64, 128), BF16), pltpu.VMEM((2, 2, 64, 128), BF16),
        pltpu.VMEM((2, 64, 128), BF16), pltpu.VMEM((2, 64, 128), BF16), pltpu.VMEM((64, 128), F32),
        pltpu.VMEM((3, 2, 64, 1024), BF16), pltpu.VMEM((3, 2, 4, 16, 1024), BF16), pltpu.VMEM((2, 64, 1024), F32),
        pltpu.VMEM((3, 2, 3, 16, 1024), BF16), pltpu.VMEM((3, 2, 3, 16, 1024), BF16), pltpu.VMEM((2, 2, 128, 1024), BF16),
        pltpu.VMEM((2, 128, 2 * units), BF16),
        dma((10,)), dma((11,)), dma((11,)), dma((3, 2, 4)), dma((3, 2, 4)), dma((3, 2, 3)), dma((3, 2, 3)),
        dma((3, 2, 4)), dma((3, 2, 4)), dma((3, 2, 3)), dma((3, 2, 3)), dma((2, 8)), dma((2, 8)),
    ]
    return pl.pallas_call(
        tail_kernel,
        out_shape=jax.ShapeDtypeStruct(x_in.shape, BF16),
        in_specs=[hbm, vmem, vmem] + [hbm] * 8 + [vmem, vmem],
        out_specs=vmem,
        scratch_shapes=scratch,
        compiler_params=pltpu.CompilerParams(collective_id=0, has_side_effects=True, vmem_limit_bytes=60 * 1024 * 1024),
        name="tail",
    )(x_in, attn, mask_t, ck_t, cv_t, wo, cq_t, co, wg_t, wu_t, wd, nc, nm)


def head_kernel(tok_ref, rb_ref, x_ref, wq_ref, wk_ref, wv_ref, ns_ref, k_hbm, v_hbm,
                attn_ref, nk_hbm, nv_hbm,
                kbuf, vbuf, h_buf, qq, k_new, v_new, table, in_sem, out_sem):
    rows, depth, t_len = kbuf.shape
    n_chunks = in_sem.shape[1]
    size = rows // n_chunks

    def chunk_copy(i, which):
        hbm, buf = ((k_hbm, kbuf), (v_hbm, vbuf))[which]
        part = pl.ds(i * size, size)
        return pltpu.make_async_copy(hbm.at[part], buf.at[part], in_sem.at[which, i])

    def chunk_out(i, which):
        hbm, buf = ((nk_hbm, kbuf), (nv_hbm, vbuf))[which]
        part = pl.ds(i * size, size)
        return pltpu.make_async_copy(buf.at[part], hbm.at[part], out_sem.at[which, i])

    for i in range(n_chunks):
        chunk_copy(i, 0).start()
        chunk_copy(i, 1).start()

    distance = lax.broadcasted_iota(jnp.int32, (t_len, t_len), 0) - lax.broadcasted_iota(jnp.int32, (t_len, t_len), 1)
    bias = jnp.full((t_len, t_len), rb_ref[0], F32)
    for bucket, edge in enumerate(BUCKET_EDGES):
        bias = jnp.where(distance >= edge, rb_ref[bucket + 1], bias)
    table[...] = jnp.where(distance >= 0, bias, NEG_FILL)

    wqq = jnp.concatenate([wq_ref[...], wq_ref[...]], axis=0)
    for i in range(rows // 128):
        part = slice(i * 128, i * 128 + 128)
        h = rms_norm(x_ref[part, :].astype(F32), ns_ref[...])
        qq[part, :] = dot_nt(h, wqq).astype(BF16).astype(F32)
        k_new[i] = dot_nt(wk_ref[...], h).astype(BF16).astype(F32)
        v_new[i] = dot_nt(wv_ref[...], h).astype(BF16).astype(F32)

    lane = lax.broadcasted_iota(jnp.int32, (depth, t_len), 1)
    row8 = lax.broadcasted_iota(jnp.int32, (8, 128), 0)
    half8 = lax.broadcasted_iota(jnp.int32, (8, 128), 1) // depth

    def step(i, carry):
        chunk_copy(i, 0).wait()
        chunk_copy(i, 1).wait()
        shift = lax.rem(i, 2) * size
        k_cols = pltpu.roll(k_new[i // 2], shift, 1)
        v_cols = pltpu.roll(v_new[i // 2], shift, 1)
        scores = []
        for g in range(size // 8):
            k8, bias8 = [], []
            for j in range(8):
                b = i * size + g * 8 + j
                pos = tok_ref[b]
                at_pos = lane == pos
                col = g * 8 + j
                k_b = jnp.where(at_pos, jnp.broadcast_to(k_cols[:, col:col + 1], (depth, t_len)), kbuf[b].astype(F32)).astype(BF16)
                v_b = jnp.where(at_pos, jnp.broadcast_to(v_cols[:, col:col + 1], (depth, t_len)), vbuf[b].astype(F32)).astype(BF16)
                kbuf[b] = k_b
                vbuf[b] = v_b
                k8.append(k_b)
                bias8.append(table[pl.ds(pos, 1), :])
            q8 = qq[pl.ds(pl.multiple_of(i * size + g * 8, 8), 8), :]
            q_diag = jnp.concatenate([jnp.where(row8 == 2 * m + half8, q8, 0.0) for m in range(4)], axis=1).astype(BF16)
            scores.append(dot_nn(q_diag, jnp.concatenate(k8, axis=0)) + jnp.concatenate(bias8, axis=0))
        chunk_out(i, 0).start()
        chunk_out(i, 1).start()
        s = jnp.concatenate(scores, axis=0)
        e = jnp.exp(s - jnp.max(s, axis=1, keepdims=True))
        p = (e / jnp.sum(e, axis=1, keepdims=True)).astype(BF16).astype(F32)
        outs = []
        for g in range(size // 8):
            p8 = p[g * 8:g * 8 + 8, :]
            p_diag = jnp.concatenate([jnp.where(row8 == j, p8, 0.0) for j in range(8)], axis=1).astype(BF16)
            v8 = jnp.concatenate([vbuf[i * size + g * 8 + j] for j in range(8)], axis=1)
            outs.append(dot_nt(p_diag, v8))
        attn_ref[pl.ds(pl.multiple_of(i * size, size), size), :] = jnp.concatenate(outs, axis=0).astype(BF16)
        return carry

    lax.fori_loop(0, n_chunks, step, 0)
    for i in range(n_chunks):
        chunk_out(i, 0).wait()
        chunk_out(i, 1).wait()


def head(tok_pos, rel_bias, x_in, wq_t, wk_t, wv_t, ns, k_t, v_t):
    hbm = pl.BlockSpec(memory_space=pltpu.HBM)
    vmem = pl.BlockSpec(memory_space=pltpu.VMEM)
    smem = pl.BlockSpec(memory_space=pltpu.SMEM)
    rows, depth, t_len = k_t.shape
    dma = pltpu.SemaphoreType.DMA
    n_chunks = 8
    return pl.pallas_call(
        head_kernel,
        out_shape=(jax.ShapeDtypeStruct((rows, depth), BF16), jax.ShapeDtypeStruct(k_t.shape, BF16), jax.ShapeDtypeStruct(v_t.shape, BF16)),
        in_specs=[smem, smem] + [vmem] * 5 + [hbm] * 2,
        out_specs=(vmem, hbm, hbm),
        scratch_shapes=[
            pltpu.VMEM(k_t.shape, BF16), pltpu.VMEM(v_t.shape, BF16), pltpu.VMEM((8, 128), BF16),
            pltpu.VMEM((rows, 2 * depth), F32), pltpu.VMEM((rows // 128, depth, 128), F32), pltpu.VMEM((rows // 128, depth, 128), F32),
            pltpu.VMEM((t_len, t_len), F32), dma((2, n_chunks)), dma((2, n_chunks)),
        ],
        compiler_params=pltpu.CompilerParams(vmem_limit_bytes=60 * 1024 * 1024),
        name="head",
    )(tok_pos, rel_bias, x_in, wq_t, wk_t, wv_t, ns, k_t, v_t)


def solution(mesh):
    def local_layer(x_in, tok_pos, self_k, self_v, cross_k, cross_v, enc_mask, rel_bias, w_q, w_k, w_v, w_o, cross_q, cross_o, w_gate, w_up, w_down, norm_self, norm_cross, norm_mlp):
        k_t = jnp.transpose(self_k[:, :, 0, :], (0, 2, 1))
        v_t = jnp.transpose(self_v[:, :, 0, :], (0, 2, 1))
        attn, new_k, new_v = head(tok_pos, rel_bias[:, 0], x_in, w_q.T, w_k.T, w_v.T, norm_self, k_t, v_t)
        new_self_k = jnp.transpose(new_k, (0, 2, 1))[:, :, None, :]
        new_self_v = jnp.transpose(new_v, (0, 2, 1))[:, :, None, :]
        ck_t = jnp.transpose(cross_k[:, :, 0, :], (1, 2, 0))
        cv_t = jnp.transpose(cross_v[:, :, 0, :], (1, 2, 0))
        out = tail(x_in, attn, enc_mask.T, ck_t, cv_t, w_o, cross_q.T, cross_o, w_gate.T, w_up.T, w_down,
                   norm_cross, norm_mlp)
        return out, new_self_k, new_self_v

    cache_spec = P('dp', None, 'tp', None)
    split_cols = P(None, 'tp')
    split_rows = P('tp', None)
    in_specs = (P('dp', None), P('dp'), cache_spec, cache_spec, cache_spec, cache_spec, P('dp', None), split_cols, split_cols, split_cols, split_cols, split_rows, split_cols, split_rows, split_cols, split_cols, split_rows, P(None), P(None), P(None))
    out_specs = (P('dp', None), cache_spec, cache_spec)
    return jax.shard_map(local_layer, mesh=mesh, in_specs=in_specs, out_specs=out_specs, check_vma=False)
```

time: 104 us -> 91.1 us (0.88); the launches traced: 104 us -> 89.6 us
  Pallas kernels: 97 us -> 86.7 us
  local copies, waits for them, and re-layouts: 6.08 us -> 2.26 us
    pallas_call x1, Pallas kernels: 81.8 us -> 71.4 us  [tail(): pl.pallas_call(tail_kernel, out_shape=jax.ShapeDtypeStruct(x_in.shape, BF...]
    broadcast_in_dim x3 -> x0, local copies, waits for them, and re-layouts: 3.82 us -> none  [the longest x1 1.27 us: local_layer(): norm_cross[None, :]]
where the time goes in v3:
time: 91.1 us; the launch traced here: 89.6 us
  Pallas kernels  86.7 us (95%)
  local copies, waits for them, and re-layouts  2.26 us (2%)
    pallas_call x1, Pallas kernels, tail(): pl.pallas_call(tail_kernel, out_shape=jax.ShapeDtypeStruct(x_in.shape, BF...  71.4 us
    pallas_call x1, Pallas kernels, head(): pl.pallas_call(head_kernel, out_shape=(jax.ShapeDtypeStruct((rows, depth)...  15.2 us
    unnamed x1, local copies, waits for them, and re-layouts  2.26 us

profile of v3, /device:TPU:0, one launch (start us, length us, event | category | flops | bytes accessed | tf_op | source)
XLA Modules:
  0.0 89.6 jit_solution(6292006404622845762)
XLA Ops:
  0.6 15.2 %head.1 = (bf16[512,64]{1,0:T(8,128)(2,1)}, bf16[512,64,128]{2,1,0:T(8,128)(2,1)}, bf16[512,64,128]{2,1,0:T(8,128)(2,1)}) custom-call(s32[512]{0:T(512)} %tok_ref.1, f32[32]{0:T(128)} %bitcast.41, bf16[512,1024]{1,0:T(8,128)(2,1)} %x_hbm.1, bf16[64,1024]{1,0:T(8,128)(2,1)} %bitcast.36, bf16[64,1024]{1,0:T(8,128)(2,1)} %bitcast.37, ...), custom_call_target="tpu_custom_call" | custom-call | tf_op jit(solution)/shard_map/head/pallas_call | solution.py:334
  15.9 71.4 %tail.1 = bf16[512,1024]{1,0:T(8,128)(2,1)} custom-call(bf16[512,1024]{1,0:T(8,128)(2,1)} %x_hbm.1, bf16[512,64]{1,0:T(8,128)(2,1)} %get-tuple-element.6.attn_ref, s32[64,512]{1,0:T(8,128)} %bitcast.39, bf16[64,64,512]{2,1,0:T(8,128)(2,1)} %bitcast.32, bf16[64,64,512]{2,1,0:T(8,128)(2,1)} %bitcast.33, bf16[64,1024]{1,0:T(8,128)(2,1)} %wo_hbm.1, ...), custom_call_target="tpu_custom_call" | custom-call | tf_op jit(solution)/shard_map/tail/pallas_call | solution.py:234
  87.3 2.3 %copy.26 = bf16[512,1024]{1,0:T(8,128)(2,1)} copy(bf16[512,1024]{1,0:T(8,128)(2,1)} %tail.1) | data formatting | bytes 2097152

commit v4 on v3

v4 whole, which is shorter than its diff:
```python
import math
import jax
import jax.numpy as jnp
from jax import lax
from jax.experimental import pallas as pl
from jax.experimental.pallas import tpu as pltpu
from jax.sharding import PartitionSpec as P

BUCKET_EDGES = tuple(range(1, 16)) + (16,) + tuple(int(math.ceil(16.0 * 8.0 ** (m / 16.0))) for m in range(1, 16))
NEG_FILL = -1e30
MESH = pl.DeviceIdType.MESH
F32 = jnp.float32
BF16 = jnp.bfloat16
K_ORDER = (2, 1, 3)


def rms_norm(values, norm_scale):
    inv_rms = lax.rsqrt(jnp.mean(values * values, axis=-1, keepdims=True) + 1e-6)
    return (values * inv_rms * norm_scale.astype(F32)[None, :]).astype(BF16)


def gelu_tanh(u):
    return u * (0.5 * (1.0 + jnp.tanh(math.sqrt(2.0 / math.pi) * (u + 0.044715 * (u * u * u)))))


def dot_nt(a, b):
    return lax.dot_general(a, b, (((1,), (1,)), ((), ())), preferred_element_type=F32)


def dot_nn(a, b):
    return jnp.dot(a, b, preferred_element_type=F32)


def tail_kernel(x_hbm, attn_ref, mask_ref, ck_hbm, cv_hbm, wo_hbm, cq_hbm, co_hbm, wg_hbm, wu_hbm, wd_hbm, woy_hbm, cqy_hbm, coy_hbm, nc_ref, nm_ref,
                out_ref,
                x_buf, ck, cv, wo4, cq4, co4, wg4, wu4, wd4, att_rcv, heads, q_snd, q_rcv, o_buf, o_rcv, scores,
                own, z_snd, z_rcv, h_buf, act,
                loc_sem, w_ssem, w_rsem, at_ssem, at_rsem, q_ssem, q_rsem, o_ssem, o_rsem, zs_sem, zr_sem, gzs_sem, gzr_sem, gys_sem, gyr_sem, cs_sem, cr_sem):
    me = lax.axis_index("tp")
    c = lax.rem(me, 2)
    y = lax.rem(me // 2, 2)
    z = me // 4
    quad = {r: {"tp": z * 4 + (y if r < 2 else 1 - y) * 2 + (c if r == 2 else 1 - c)} for r in (1, 2, 3)}
    quad_c = {0: c, 1: 1 - c, 2: c, 3: 1 - c}
    quad_y = {0: y, 1: y, 2: 1 - y, 3: 1 - y}
    z_peer = {k: {"tp": lax.rem(z + k, 4) * 4 + y * 2 + c} for k in (1, 2, 3)}
    sends = []

    def remote(src, dst, ssem, rsem, peer):
        return pltpu.make_async_remote_copy(src_ref=src, dst_ref=dst, send_sem=ssem, recv_sem=rsem, device_id=peer, device_id_type=MESH)

    def start(src, dst, ssem, rsem, peer):
        copy = remote(src, dst, ssem, rsem, peer)
        copy.start()
        sends.append(copy)
        return copy

    def span(base, size):
        return pl.ds(pl.multiple_of(base, size), size)

    def chunk(base, zz):
        return span(base + zz * 16, 16)

    def slot(ref, r):
        size = ref.shape[0] // 4
        return ref.at[pl.ds(r * size, size)]

    local = [pltpu.make_async_copy(src, dst, loc_sem.at[i]) for i, (src, dst) in enumerate((
        (x_hbm.at[chunk(c * 256 + y * 64, z)], x_buf.at[0]),
        (x_hbm.at[chunk(c * 256 + 128 + y * 64, z)], x_buf.at[1]),
        (wo_hbm, slot(wo4, 0)), (woy_hbm, slot(wo4, 2)),
        (cq_hbm, slot(cq4, 0)), (cqy_hbm, slot(cq4, 2)),
        (ck_hbm, ck), (cv_hbm, cv),
        (co_hbm, slot(co4, 0)), (coy_hbm, slot(co4, 2)),
        (wg_hbm, slot(wg4, 0)), (wu_hbm, slot(wu4, 0)), (wd_hbm, slot(wd4, 0)),
    ))]
    for copy in local:
        copy.start()

    barrier = pltpu.get_barrier_semaphore()
    for peer in (quad[1], quad[2], quad[3], z_peer[1], z_peer[2], z_peer[3]):
        pl.semaphore_signal(barrier, inc=1, device_id=peer, device_id_type=MESH)
    pl.semaphore_wait(barrier, 6)

    def rows_of(b, r):
        return span(quad_c[r] * 256 + b * 128 + quad_y[r] * 64, 64)

    att = {}
    for b in range(2):
        for r in (3, 2, 1):
            att[b, r] = start(attn_ref.at[rows_of(b, r)], att_rcv.at[b, r - 1], at_ssem.at[b, r - 1], at_rsem.at[b, r - 1], quad[r])
    to_core = {}
    for i, (src, dst, r) in enumerate((
        (wo_hbm, wo4, 1), (woy_hbm, wo4, 3), (cq_hbm, cq4, 1), (cqy_hbm, cq4, 3), (co_hbm, co4, 1), (coy_hbm, co4, 3),
        (wg_hbm, wg4, 1), (wu_hbm, wu4, 1), (wd_hbm, wd4, 1),
    )):
        to_core[i] = start(src, slot(dst, r), w_ssem.at[i], w_rsem.at[i], quad[1])
    wg_y = start(wg_hbm, slot(wg4, 2), w_ssem.at[9], w_rsem.at[9], quad[2])
    wu_y = start(wu_hbm, slot(wu4, 2), w_ssem.at[10], w_rsem.at[10], quad[2])
    late = {}

    def start_wd():
        late["wd"] = start(wd_hbm, slot(wd4, 2), w_ssem.at[11], w_rsem.at[11], quad[2])

    def forward_gate_up():
        wg_y.wait_recv()
        late["wg"] = start(slot(wg4, 2), slot(wg4, 3), w_ssem.at[12], w_rsem.at[12], quad[1])
        wu_y.wait_recv()
        late["wu"] = start(slot(wu4, 2), slot(wu4, 3), w_ssem.at[13], w_rsem.at[13], quad[1])

    def forward_wd():
        late["wd"].wait_recv()
        late["wd3"] = start(slot(wd4, 2), slot(wd4, 3), w_ssem.at[14], w_rsem.at[14], quad[1])

    waited = set()

    def once(name, *waits):
        if name not in waited:
            waited.add(name)
            for wait in waits:
                wait()

    def reduce_scatter(p, b, partial):
        own[b] = partial
        z_snd[p, b] = partial.astype(BF16)
        copies = {}
        for k in K_ORDER:
            copies[k] = start(z_snd.at[p, b, chunk(0, lax.rem(z + k, 4))], z_rcv.at[p, b, k - 1], zs_sem.at[p, b, k - 1], zr_sem.at[p, b, k - 1], z_peer[k])
        yield
        total = own[b, chunk(0, z)]
        for k in (1, 3, 2):
            copies[k].wait_recv()
            total = total + z_rcv[p, b, k - 1].astype(F32)
        return total

    def gather_start(p, b, mine):
        for k in K_ORDER:
            start(mine, mine, gzs_sem.at[p, b, k - 1], gzr_sem.at[p, b, k - 1], z_peer[k])

    def gather_wait(p, b, part, k):
        remote(part, part, gzs_sem.at[p, b, k - 1], gzr_sem.at[p, b, k - 1], z_peer[k]).wait_recv()

    def gather(p, b):
        buf = h_buf.at[p, b]
        gather_start(p, b, buf.at[chunk(0, z)])
        yield
        for k in (1, 3, 2):
            gather_wait(p, b, buf.at[chunk(0, lax.rem(z + 4 - k, 4))], k)

    def gather_out(b):
        first = c * 256 + b * 128

        def part_at(yy, k):
            return out_ref.at[chunk(first + yy * 64, lax.rem(z + 4 - k, 4))]

        def pass_on(part, s):
            start(part, part, cs_sem.at[b, s], cr_sem.at[b, s], quad[1])

        mine = part_at(y, 0)
        start(mine, mine, gys_sem.at[b, 0], gyr_sem.at[b, 0], quad[2])
        gather_start(2, b, mine)
        pass_on(mine, 0)
        yield
        for k in (1, 3, 2):
            part = part_at(y, k)
            gather_wait(2, b, part, k)
            start(part, part, gys_sem.at[b, k], gyr_sem.at[b, k], quad[2])
            pass_on(part, k)
        yield
        for k in (0, 1, 3, 2):
            part = part_at(1 - y, k)
            remote(part, part, gys_sem.at[b, k], gyr_sem.at[b, k], quad[2]).wait_recv()
            pass_on(part, 4 + k)

    def cross(half_id, b):
        lanes = span(half_id * 256 + b * 128, 128)
        q_blk = q_rcv[b, half_id].astype(F32).T

        def score_step(i, carry):
            rows = span(i * 8, 8)
            scores[rows, :] = jnp.sum(ck[rows, :, lanes].astype(F32) * q_blk[None], axis=1)
            return carry

        lax.fori_loop(0, 8, score_step, 0)
        s = scores[...] + jnp.where(mask_ref[:, lanes] != 0, 0.0, NEG_FILL)
        e = jnp.exp(s - jnp.max(s, axis=0, keepdims=True))
        scores[...] = (e / jnp.sum(e, axis=0, keepdims=True)).astype(BF16).astype(F32)

        def mix_step(i, acc):
            p_blk = scores[span(i * 8, 8), :]
            for j in range(8):
                acc = acc + cv[i * 8 + j, :, lanes].astype(F32) * p_blk[j:j + 1, :]
            return acc

        return lax.fori_loop(0, 8, mix_step, jnp.zeros((64, 128), F32)).T.astype(BF16)

    def flow(b):
        for r in (1, 2, 3):
            att[b, r].wait_recv()
        heads[b] = jnp.concatenate([attn_ref[rows_of(b, 0), :]] + [att_rcv[b, r] for r in range(3)], axis=1)
        once("wo", local[2].wait, local[3].wait, to_core[0].wait_recv, to_core[1].wait_recv)
        total = yield from reduce_scatter(0, b, dot_nn(heads[b], wo4[...]))
        local[b].wait()
        resid = x_buf[b].astype(F32) + total
        h_buf[0, b, chunk(0, z)] = rms_norm(resid, nc_ref[...])
        yield from gather(0, b)
        once("cq", local[4].wait, local[5].wait, to_core[2].wait_recv, to_core[3].wait_recv)
        q4 = dot_nt(h_buf[0, b], cq4[...]).astype(BF16)
        for r in (3, 2, 1):
            q_snd[b, r - 1] = q4[:, r * 64:r * 64 + 64]
            start(q_snd.at[b, r - 1], q_rcv.at[b, c, span(y * 64, 64)], q_ssem.at[b, r - 1], q_rsem.at[b, r - 1], quad[r])
        q_rcv[b, c, span(y * 64, 64)] = q4[:, 0:64]
        yield
        once("kv", local[6].wait, local[7].wait)
        for half_id, pieces in ((c, (2,)), (1 - c, (1, 3))):
            for r in pieces:
                remote(q_snd.at[b, r - 1], q_rcv.at[b, quad_c[r], span(quad_y[r] * 64, 64)], q_ssem.at[b, r - 1], q_rsem.at[b, r - 1], quad[r]).wait_recv()
            o_buf[b, half_id] = cross(half_id, b)
            for r in reversed(pieces):
                start(o_buf.at[b, half_id, span(quad_y[r] * 64, 64)], o_rcv.at[b, r - 1], o_ssem.at[b, r - 1], o_rsem.at[b, r - 1], quad[r])
        if b == 1:
            start_wd()
        yield
        for r in (1, 2, 3):
            remote(o_buf.at[b, quad_c[r], span(quad_y[r] * 64, 64)], o_rcv.at[b, r - 1], o_ssem.at[b, r - 1], o_rsem.at[b, r - 1], quad[r]).wait_recv()
        heads[b] = jnp.concatenate([o_buf[b, c, span(y * 64, 64), :]] + [o_rcv[b, r] for r in range(3)], axis=1)
        once("co", local[8].wait, local[9].wait, to_core[4].wait_recv, to_core[5].wait_recv)
        partial = dot_nn(heads[b], co4[...])
        if b == 1:
            forward_gate_up()
        total = yield from reduce_scatter(1, b, partial)
        resid = resid + total
        h_buf[1, b, chunk(0, z)] = rms_norm(resid, nm_ref[...])
        yield from gather(1, b)
        if b == 0:
            forward_wd()
        once("gu", local[10].wait, local[11].wait, to_core[6].wait_recv, to_core[7].wait_recv, late["wg"].wait_recv, late["wu"].wait_recv)
        h = h_buf[1, b]
        act[b] = (gelu_tanh(dot_nt(h, wg4[...])) * dot_nt(h, wu4[...])).astype(BF16)
        once("wd", local[12].wait, to_core[8].wait_recv, late["wd3"].wait_recv)
        total = yield from reduce_scatter(2, b, dot_nn(act[b], wd4[...]))
        resid = resid + total
        out_ref[chunk(c * 256 + b * 128 + y * 64, z)] = resid.astype(BF16)
        yield from gather_out(b)

    flows = [flow(0), flow(1)]
    while flows:
        for item in list(flows):
            try:
                next(item)
            except StopIteration:
                flows.remove(item)
    for b in range(2):
        for s in range(8):
            yy = y if s < 4 else 1 - y
            part = out_ref.at[chunk((1 - c) * 256 + b * 128 + yy * 64, lax.rem(z + 4 - s % 4, 4))]
            remote(part, part, cs_sem.at[b, s], cr_sem.at[b, s], quad[1]).wait_recv()
    for copy in sends:
        copy.wait_send()


def tail(x_in, attn, mask_t, ck_t, cv_t, wo, cq_t, co, wg_t, wu_t, wd, woy, cqy_t, coy, nc, nm):
    hbm = pl.BlockSpec(memory_space=pltpu.HBM)
    anywhere = pl.BlockSpec(memory_space=pl.ANY)
    vmem = pl.BlockSpec(memory_space=pltpu.VMEM)
    units = wd.shape[0]
    dma = pltpu.SemaphoreType.DMA
    quarter = (256, 1024)
    scratch = [
        pltpu.VMEM((2, 16, 1024), BF16), pltpu.VMEM(ck_t.shape, BF16), pltpu.VMEM(cv_t.shape, BF16),
        pltpu.VMEM(quarter, BF16), pltpu.VMEM(quarter, BF16), pltpu.VMEM(quarter, BF16),
        pltpu.VMEM((4 * units, 1024), BF16), pltpu.VMEM((4 * units, 1024), BF16), pltpu.VMEM((4 * units, 1024), BF16),
        pltpu.VMEM((2, 3, 64, 64), BF16), pltpu.VMEM((2, 64, 256), BF16), pltpu.VMEM((2, 3, 64, 64), BF16), pltpu.VMEM((2, 2, 128, 64), BF16),
        pltpu.VMEM((2, 2, 128, 64), BF16), pltpu.VMEM((2, 3, 64, 64), BF16), pltpu.VMEM((64, 128), F32),
        pltpu.VMEM((2, 64, 1024), F32), pltpu.VMEM((3, 2, 64, 1024), BF16), pltpu.VMEM((3, 2, 3, 16, 1024), BF16), pltpu.VMEM((2, 2, 64, 1024), BF16),
        pltpu.VMEM((2, 64, 4 * units), BF16),
        dma((13,)), dma((15,)), dma((15,)), dma((2, 3)), dma((2, 3)), dma((2, 3)), dma((2, 3)), dma((2, 3)), dma((2, 3)),
        dma((3, 2, 3)), dma((3, 2, 3)), dma((3, 2, 3)), dma((3, 2, 3)), dma((2, 4)), dma((2, 4)), dma((2, 8)), dma((2, 8)),
    ]
    return pl.pallas_call(
        tail_kernel,
        out_shape=jax.ShapeDtypeStruct(x_in.shape, BF16),
        in_specs=[hbm, vmem, vmem] + [hbm] * 8 + [anywhere] * 3 + [vmem, vmem],
        out_specs=vmem,
        scratch_shapes=scratch,
        compiler_params=pltpu.CompilerParams(collective_id=0, has_side_effects=True, vmem_limit_bytes=60 * 1024 * 1024),
        name="tail",
    )(x_in, attn, mask_t, ck_t, cv_t, wo, cq_t, co, wg_t, wu_t, wd, woy, cqy_t, coy, nc, nm)


def head_kernel(tok_ref, rb_ref, x_ref, wq_ref, wk_ref, wv_ref, ns_ref, k_hbm, v_hbm,
                attn_ref, nk_hbm, nv_hbm,
                kbuf, vbuf, h_buf, qq, k_new, v_new, table, in_sem, out_sem):
    rows, depth, t_len = kbuf.shape
    n_chunks = in_sem.shape[1]
    size = rows // n_chunks

    def chunk_copy(i, which):
        hbm, buf = ((k_hbm, kbuf), (v_hbm, vbuf))[which]
        part = pl.ds(i * size, size)
        return pltpu.make_async_copy(hbm.at[part], buf.at[part], in_sem.at[which, i])

    def chunk_out(i, which):
        hbm, buf = ((nk_hbm, kbuf), (nv_hbm, vbuf))[which]
        part = pl.ds(i * size, size)
        return pltpu.make_async_copy(buf.at[part], hbm.at[part], out_sem.at[which, i])

    for i in range(n_chunks):
        chunk_copy(i, 0).start()
        chunk_copy(i, 1).start()

    distance = lax.broadcasted_iota(jnp.int32, (t_len, t_len), 0) - lax.broadcasted_iota(jnp.int32, (t_len, t_len), 1)
    bias = jnp.full((t_len, t_len), rb_ref[0], F32)
    for bucket, edge in enumerate(BUCKET_EDGES):
        bias = jnp.where(distance >= edge, rb_ref[bucket + 1], bias)
    table[...] = jnp.where(distance >= 0, bias, NEG_FILL)

    wqq = jnp.concatenate([wq_ref[...], wq_ref[...]], axis=0)
    for i in range(rows // 128):
        part = slice(i * 128, i * 128 + 128)
        h = rms_norm(x_ref[part, :].astype(F32), ns_ref[...])
        qq[part, :] = dot_nt(h, wqq).astype(BF16).astype(F32)
        k_new[i] = dot_nt(wk_ref[...], h).astype(BF16).astype(F32)
        v_new[i] = dot_nt(wv_ref[...], h).astype(BF16).astype(F32)

    lane = lax.broadcasted_iota(jnp.int32, (depth, t_len), 1)
    row8 = lax.broadcasted_iota(jnp.int32, (8, 128), 0)
    half8 = lax.broadcasted_iota(jnp.int32, (8, 128), 1) // depth

    def step(i, carry):
        chunk_copy(i, 0).wait()
        chunk_copy(i, 1).wait()
        shift = lax.rem(i, 2) * size
        k_cols = pltpu.roll(k_new[i // 2], shift, 1)
        v_cols = pltpu.roll(v_new[i // 2], shift, 1)
        scores = []
        for g in range(size // 8):
            k8, bias8 = [], []
            for j in range(8):
                b = i * size + g * 8 + j
                pos = tok_ref[b]
                at_pos = lane == pos
                col = g * 8 + j
                k_b = jnp.where(at_pos, jnp.broadcast_to(k_cols[:, col:col + 1], (depth, t_len)), kbuf[b].astype(F32)).astype(BF16)
                v_b = jnp.where(at_pos, jnp.broadcast_to(v_cols[:, col:col + 1], (depth, t_len)), vbuf[b].astype(F32)).astype(BF16)
                kbuf[b] = k_b
                vbuf[b] = v_b
                k8.append(k_b)
                bias8.append(table[pl.ds(pos, 1), :])
            q8 = qq[pl.ds(pl.multiple_of(i * size + g * 8, 8), 8), :]
            q_diag = jnp.concatenate([jnp.where(row8 == 2 * m + half8, q8, 0.0) for m in range(4)], axis=1).astype(BF16)
            scores.append(dot_nn(q_diag, jnp.concatenate(k8, axis=0)) + jnp.concatenate(bias8, axis=0))
        chunk_out(i, 0).start()
        chunk_out(i, 1).start()
        s = jnp.concatenate(scores, axis=0)
        e = jnp.exp(s - jnp.max(s, axis=1, keepdims=True))
        p = (e / jnp.sum(e, axis=1, keepdims=True)).astype(BF16).astype(F32)
        outs = []
        for g in range(size // 8):
            p8 = p[g * 8:g * 8 + 8, :]
            p_diag = jnp.concatenate([jnp.where(row8 == j, p8, 0.0) for j in range(8)], axis=1).astype(BF16)
            v8 = jnp.concatenate([vbuf[i * size + g * 8 + j] for j in range(8)], axis=1)
            outs.append(dot_nt(p_diag, v8))
        attn_ref[pl.ds(pl.multiple_of(i * size, size), size), :] = jnp.concatenate(outs, axis=0).astype(BF16)
        return carry

    lax.fori_loop(0, n_chunks, step, 0)
    for i in range(n_chunks):
        chunk_out(i, 0).wait()
        chunk_out(i, 1).wait()


def head(tok_pos, rel_bias, x_in, wq_t, wk_t, wv_t, ns, k_t, v_t):
    hbm = pl.BlockSpec(memory_space=pltpu.HBM)
    vmem = pl.BlockSpec(memory_space=pltpu.VMEM)
    smem = pl.BlockSpec(memory_space=pltpu.SMEM)
    rows, depth, t_len = k_t.shape
    dma = pltpu.SemaphoreType.DMA
    n_chunks = 8
    return pl.pallas_call(
        head_kernel,
        out_shape=(jax.ShapeDtypeStruct((rows, depth), BF16), jax.ShapeDtypeStruct(k_t.shape, BF16), jax.ShapeDtypeStruct(v_t.shape, BF16)),
        in_specs=[smem, smem] + [vmem] * 5 + [hbm] * 2,
        out_specs=(vmem, hbm, hbm),
        scratch_shapes=[
            pltpu.VMEM(k_t.shape, BF16), pltpu.VMEM(v_t.shape, BF16), pltpu.VMEM((8, 128), BF16),
            pltpu.VMEM((rows, 2 * depth), F32), pltpu.VMEM((rows // 128, depth, 128), F32), pltpu.VMEM((rows // 128, depth, 128), F32),
            pltpu.VMEM((t_len, t_len), F32), dma((2, n_chunks)), dma((2, n_chunks)),
        ],
        compiler_params=pltpu.CompilerParams(vmem_limit_bytes=60 * 1024 * 1024),
        cost_estimate=pl.CostEstimate(flops=4 * 10**9, bytes_accessed=34 * 1024 * 1024, transcendentals=65536),
        name="head",
    )(tok_pos, rel_bias, x_in, wq_t, wk_t, wv_t, ns, k_t, v_t)


def solution(mesh):
    def local_layer(x_in, tok_pos, self_k, self_v, cross_k, cross_v, enc_mask, rel_bias, w_q, w_k, w_v, w_o, cross_q, cross_o, w_gate, w_up, w_down, norm_self, norm_cross, norm_mlp):
        k_t = jnp.transpose(self_k[:, :, 0, :], (0, 2, 1))
        v_t = jnp.transpose(self_v[:, :, 0, :], (0, 2, 1))
        attn, new_k, new_v = head(tok_pos, rel_bias[:, 0], x_in, w_q.T, w_k.T, w_v.T, norm_self, k_t, v_t)
        new_self_k = jnp.transpose(new_k, (0, 2, 1))[:, :, None, :]
        new_self_v = jnp.transpose(new_v, (0, 2, 1))[:, :, None, :]
        ck_t = jnp.transpose(cross_k[:, :, 0, :], (1, 2, 0))
        cv_t = jnp.transpose(cross_v[:, :, 0, :], (1, 2, 0))
        tp_size = mesh.shape["tp"]
        across_y = [(i, i ^ 2) for i in range(tp_size)]
        wo_y, cq_y, co_y = (lax.ppermute(w, "tp", across_y) for w in (w_o, cross_q.T, cross_o))
        out = tail(x_in, attn, enc_mask.T, ck_t, cv_t, w_o, cross_q.T, cross_o, w_gate.T, w_up.T, w_down, wo_y, cq_y, co_y,
                   norm_cross, norm_mlp)
        return out, new_self_k, new_self_v

    cache_spec = P('dp', None, 'tp', None)
    split_cols = P(None, 'tp')
    split_rows = P('tp', None)
    in_specs = (P('dp', None), P('dp'), cache_spec, cache_spec, cache_spec, cache_spec, P('dp', None), split_cols, split_cols, split_cols, split_cols, split_rows, split_cols, split_rows, split_cols, split_cols, split_rows, P(None), P(None), P(None))
    out_specs = (P('dp', None), cache_spec, cache_spec)
    return jax.shard_map(local_layer, mesh=mesh, in_specs=in_specs, out_specs=out_specs, check_vma=False)
```

time: 91.1 us -> 86.1 us (0.945); the launches traced: 89.6 us -> 85.9 us
  Pallas kernels: 86.7 us -> 77.1 us
  starting transfers between devices: 0 us -> 5.12 us
    pallas_call x1, Pallas kernels: 71.4 us -> 61.9 us  [tail(): pl.pallas_call(tail_kernel, out_shape=jax.ShapeDtypeStruct(x_in.shape, BF...]
    ppermute x0 -> x3, starting transfers between devices: none -> 5.12 us  [local_layer(): lax.ppermute(w, 'tp', across_y)]
    unnamed x1 -> x7, local copies, waits for them, and re-layouts: 2.26 us -> 2.99 us
  transfers between devices with their start and end apart: 0 -> 3, of which waited for: 0 -> 0; matrix products, arithmetic and copies ran while one was open for 0% -> 0% of each run, Pallas kernels for 0% -> 18%
where the time goes in v4:
time: 86.1 us; the launch traced here: 85.9 us
  Pallas kernels  77.1 us (90%)
  starting transfers between devices  5.12 us (6%)
  local copies, waits for them, and re-layouts  2.99 us (3%)
    pallas_call x1, Pallas kernels, tail(): pl.pallas_call(tail_kernel, out_shape=jax.ShapeDtypeStruct(x_in.shape, BF...  61.9 us
    pallas_call x1, Pallas kernels, head(): pl.pallas_call(head_kernel, out_shape=(jax.ShapeDtypeStruct((rows, depth)...  15.2 us
    ppermute x3, starting transfers between devices, local_layer(): lax.ppermute(w, 'tp', across_y)  5.12 us
    unnamed x7, local copies, waits for them, and re-layouts  2.99 us
  transfers between devices with their start and end apart: 3, of which 0 were waited for; matrix products, arithmetic and copies ran while one was open for 0% of the time, Pallas kernels for 18%

profile of v4, /device:TPU:0, one launch (start us, length us, event | category | flops | bytes accessed | tf_op | source)
XLA Modules:
  0.0 85.9 jit_solution(7058514443249225091)
XLA Ops:
  0.6 3.1 %collective-permute-start.1 = (bf16[64,1024]{1,0:T(8,128)(2,1)}, bf16[64,1024]{1,0:T(8,128)(2,1)S(1)}, u32[]{:S(2)}, u32[]{:S(2)}) collective-permute-start(bf16[64,1024]{1,0:T(8,128)(2,1)} %bitcast.40), channel_id=1, source_target_pairs={{0,2},{1,3},{2,0},{3,1},{4,6},{5,7},{6,4},{7,5},{8,10},{9,11},{10,... | collective-permute-start | bytes 393224 | tf_op jit(solution)/shard_map/ppermute | solution.py:407
  3.7 0.1 collective-permute-start
  3.8 1.9 %collective-permute-start.2 = (bf16[64,1024]{1,0:T(8,128)(2,1)}, bf16[64,1024]{1,0:T(8,128)(2,1)S(1)}, u32[]{:S(2)}, u32[]{:S(2)}) collective-permute-start(bf16[64,1024]{1,0:T(8,128)(2,1)} %co_hbm.1), channel_id=1, source_target_pairs={{0,2},{1,3},{2,0},{3,1},{4,6},{5,7},{6,4},{7,5},{8,10},{9,11},{10,... | collective-permute-start | bytes 393224 | tf_op jit(solution)/shard_map/ppermute | solution.py:407
  5.8 15.2 %head.1 = (bf16[512,64]{1,0:T(8,128)(2,1)}, bf16[512,64,128]{2,1,0:T(8,128)(2,1)}, bf16[512,64,128]{2,1,0:T(8,128)(2,1)}) custom-call(s32[512]{0:T(512)} %tok_ref.1, f32[32]{0:T(128)} %bitcast.42, bf16[512,1024]{1,0:T(8,128)(2,1)} %x_hbm.1, bf16[64,1024]{1,0:T(8,128)(2,1)} %bitcast.36, bf16[64,1024]{1,0:T(8,128)(2,1)} %bitcast.37, ...), custom_call_target="tpu_custom_call" | custom-call | flops 4000000000 | bytes 35651584 | tf_op jit(solution)/shard_map/head/pallas_call | solution.py:380
  21.0 0.0 collective-permute-done.1.cqy_hbm
  21.0 0.0 copy-start
  21.0 0.0 collective-permute-done.woy_hbm
  21.0 0.0 copy-start.1
  21.0 0.0 collective-permute-done.2.coy_hbm
  21.0 0.0 copy-start.2
  21.0 0.6 copy-done
  21.6 0.1 copy-done.1
  21.7 0.1 copy-done.2
  21.8 61.9 %tail.1 = bf16[512,1024]{1,0:T(8,128)(2,1)} custom-call(bf16[512,1024]{1,0:T(8,128)(2,1)} %x_hbm.1, bf16[512,64]{1,0:T(8,128)(2,1)} %get-tuple-element.6.attn_ref, s32[64,512]{1,0:T(8,128)} %bitcast.39, bf16[64,64,512]{2,1,0:T(8,128)(2,1)} %bitcast.32, bf16[64,64,512]{2,1,0:T(8,128)(2,1)} %bitcast.33, bf16[64,1024]{1,0:T(8,128)(2,1)} %wo_hbm.1, ...), custom_call_target="tpu_custom_call" | custom-call | tf_op jit(solution)/shard_map/tail/pallas_call | solution.py:280
  83.7 2.3 %copy.26 = bf16[512,1024]{1,0:T(8,128)(2,1)} copy(bf16[512,1024]{1,0:T(8,128)(2,1)} %tail.1) | data formatting | bytes 2097152
Async XLA Ops:
  0.6 20.3 %collective-permute-start.1 = (bf16[64,1024]{1,0:T(8,128)(2,1)}, bf16[64,1024]{1,0:T(8,128)(2,1)S(1)}, u32[]{:S(2)}, u32[]{:S(2)}) collective-permute-start(bf16[64,1024]{1,0:T(8,128)(2,1)} %bitcast.40), channel_id=1, source_target_pairs={{0,2},{1,3},{2,0},{3,1},{4,6},{5,7},{6,4},{7,5},{8,10},{9,11},{10,... | collective-permute-start | bytes 393224 | tf_op jit(solution)/shard_map/ppermute | solution.py:407
  3.7 17.3 %collective-permute-start = (bf16[64,1024]{1,0:T(8,128)(2,1)}, bf16[64,1024]{1,0:T(8,128)(2,1)S(1)}, u32[]{:S(2)}, u32[]{:S(2)}) collective-permute-start(bf16[64,1024]{1,0:T(8,128)(2,1)} %wo_hbm.1), channel_id=1, source_target_pairs={{0,2},{1,3},{2,0},{3,1},{4,6},{5,7},{6,4},{7,5},{8,10},{9,11},{10,... | collective-permute-start | bytes 393224 | tf_op jit(solution)/shard_map/ppermute | solution.py:407
  3.8 17.2 %collective-permute-start.2 = (bf16[64,1024]{1,0:T(8,128)(2,1)}, bf16[64,1024]{1,0:T(8,128)(2,1)S(1)}, u32[]{:S(2)}, u32[]{:S(2)}) collective-permute-start(bf16[64,1024]{1,0:T(8,128)(2,1)} %co_hbm.1), channel_id=1, source_target_pairs={{0,2},{1,3},{2,0},{3,1},{4,6},{5,7},{6,4},{7,5},{8,10},{9,11},{10,... | collective-permute-start | bytes 393224 | tf_op jit(solution)/shard_map/ppermute | solution.py:407
  21.0 0.7 copy-start
  21.0 0.7 copy-start.1
  21.0 0.7 copy-start.2

commit v5 on v4

--- a/solution.py
+++ b/solution.py
@@ -12,6 +12,8 @@
 F32 = jnp.float32
 BF16 = jnp.bfloat16
 K_ORDER = (2, 1, 3)
+Y_FIRST, Y_SECOND, Y_THIRD = ("cq", "co", "wg"), ("wu",), ("wv", "wd")
+VMEM_BYTES = 60 * 1024 * 1024
 
 
 def rms_norm(values, norm_scale):
@@ -31,11 +33,11 @@
     return jnp.dot(a, b, preferred_element_type=F32)
 
 
-def tail_kernel(x_hbm, attn_ref, mask_ref, ck_hbm, cv_hbm, wo_hbm, cq_hbm, co_hbm, wg_hbm, wu_hbm, wd_hbm, woy_hbm, cqy_hbm, coy_hbm, nc_ref, nm_ref,
+def tail_kernel(x_hbm, attn_ref, mask_ref, ck_hbm, cv_hbm, wo_ref, cq_hbm, co_hbm, wg_hbm, wu_hbm, wd_hbm, woy_hbm, nc_ref, nm_ref,
                 out_ref,
                 x_buf, ck, cv, wo4, cq4, co4, wg4, wu4, wd4, att_rcv, heads, q_snd, q_rcv, o_buf, o_rcv, scores,
                 own, z_snd, z_rcv, h_buf, act,
-                loc_sem, w_ssem, w_rsem, at_ssem, at_rsem, q_ssem, q_rsem, o_ssem, o_rsem, zs_sem, zr_sem, gzs_sem, gzr_sem, gys_sem, gyr_sem, cs_sem, cr_sem):
+                loc_sem, wo_ssem, wo_rsem, w_ssem, w_rsem, at_ssem, at_rsem, q_ssem, q_rsem, o_ssem, o_rsem, zs_sem, zr_sem, gzs_sem, gzr_sem, gys_sem, gyr_sem, cs_sem, cr_sem):
     me = lax.axis_index("tp")
     c = lax.rem(me, 2)
     y = lax.rem(me // 2, 2)
@@ -68,10 +70,7 @@
     local = [pltpu.make_async_copy(src, dst, loc_sem.at[i]) for i, (src, dst) in enumerate((
         (x_hbm.at[chunk(c * 256 + y * 64, z)], x_buf.at[0]),
         (x_hbm.at[chunk(c * 256 + 128 + y * 64, z)], x_buf.at[1]),
-        (wo_hbm, slot(wo4, 0)), (woy_hbm, slot(wo4, 2)),
-        (cq_hbm, slot(cq4, 0)), (cqy_hbm, slot(cq4, 2)),
-        (ck_hbm, ck), (cv_hbm, cv),
-        (co_hbm, slot(co4, 0)), (coy_hbm, slot(co4, 2)),
+        (wo_ref, slot(wo4, 0)), (woy_hbm, slot(wo4, 2)), (cq_hbm, slot(cq4, 0)), (ck_hbm, ck), (cv_hbm, cv), (co_hbm, slot(co4, 0)),
         (wg_hbm, slot(wg4, 0)), (wu_hbm, slot(wu4, 0)), (wd_hbm, slot(wd4, 0)),
     ))]
     for copy in local:
@@ -89,43 +88,44 @@
     for b in range(2):
         for r in (3, 2, 1):
             att[b, r] = start(attn_ref.at[rows_of(b, r)], att_rcv.at[b, r - 1], at_ssem.at[b, r - 1], at_rsem.at[b, r - 1], quad[r])
-    to_core = {}
-    for i, (src, dst, r) in enumerate((
-        (wo_hbm, wo4, 1), (woy_hbm, wo4, 3), (cq_hbm, cq4, 1), (cqy_hbm, cq4, 3), (co_hbm, co4, 1), (coy_hbm, co4, 3),
-        (wg_hbm, wg4, 1), (wu_hbm, wu4, 1), (wd_hbm, wd4, 1),
-    )):
-        to_core[i] = start(src, slot(dst, r), w_ssem.at[i], w_rsem.at[i], quad[1])
-    wg_y = start(wg_hbm, slot(wg4, 2), w_ssem.at[9], w_rsem.at[9], quad[2])
-    wu_y = start(wu_hbm, slot(wu4, 2), w_ssem.at[10], w_rsem.at[10], quad[2])
-    late = {}
-
-    def start_wd():
-        late["wd"] = start(wd_hbm, slot(wd4, 2), w_ssem.at[11], w_rsem.at[11], quad[2])
-
-    def forward_gate_up():
-        wg_y.wait_recv()
-        late["wg"] = start(slot(wg4, 2), slot(wg4, 3), w_ssem.at[12], w_rsem.at[12], quad[1])
-        wu_y.wait_recv()
-        late["wu"] = start(slot(wu4, 2), slot(wu4, 3), w_ssem.at[13], w_rsem.at[13], quad[1])
-
-    def forward_wd():
-        late["wd"].wait_recv()
-        late["wd3"] = start(slot(wd4, 2), slot(wd4, 3), w_ssem.at[14], w_rsem.at[14], quad[1])
-
-    waited = set()
-
-    def once(name, *waits):
-        if name not in waited:
-            waited.add(name)
-            for wait in waits:
-                wait()
-
-    def reduce_scatter(p, b, partial):
+    part = 96
+    pieces = {
+        "cq": (cq_hbm, cq4, 0, cq_hbm.shape[0]), "co": (co_hbm, co4, 0, co_hbm.shape[0]),
+        "wg": (wg_hbm, wg4, 0, wg_hbm.shape[0]), "wu": (wu_hbm, wu4, 0, part), "wv": (wu_hbm, wu4, part, wu_hbm.shape[0] - part),
+        "wd": (wd_hbm, wd4, 0, wd_hbm.shape[0]),
+    }
+    w_copy = {}
+
+    def send_weight(name, r):
+        src, slots, first, size = pieces[name]
+        rows = pl.ds(first, size)
+        if r == 3:
+            w_copy[name, 2].wait_recv()
+            src = slot(slots, 2)
+        i = list(pieces).index(name)
+        w_copy[name, r] = start(src.at[rows], slot(slots, r).at[rows], w_ssem.at[i, r - 1], w_rsem.at[i, r - 1], quad[2 if r == 2 else 1])
+
+    def weight_waits(*names):
+        return [w_copy[name, r].wait_recv for name in names for r in (1, 3)]
+
+    wo_copies = [start(src, slot(wo4, r), wo_ssem.at[r // 2], wo_rsem.at[r // 2], quad[1]) for src, r in ((wo_ref, 1), (woy_hbm, 3))]
+    for name in pieces:
+        send_weight(name, 1)
+    for name in Y_FIRST:
+        send_weight(name, 2)
+
+    def once(*waits):
+        for wait in waits:
+            wait()
+
+    def reduce_scatter(p, b, partial, then=None):
         own[b] = partial
         z_snd[p, b] = partial.astype(BF16)
         copies = {}
         for k in K_ORDER:
             copies[k] = start(z_snd.at[p, b, chunk(0, lax.rem(z + k, 4))], z_rcv.at[p, b, k - 1], zs_sem.at[p, b, k - 1], zr_sem.at[p, b, k - 1], z_peer[k])
+        if then is not None:
+            then()
         yield
         total = own[b, chunk(0, z)]
         for k in (1, 3, 2):
@@ -140,9 +140,11 @@
     def gather_wait(p, b, part, k):
         remote(part, part, gzs_sem.at[p, b, k - 1], gzr_sem.at[p, b, k - 1], z_peer[k]).wait_recv()
 
-    def gather(p, b):
+    def gather(p, b, then=None):
         buf = h_buf.at[p, b]
         gather_start(p, b, buf.at[chunk(0, z)])
+        if then is not None:
+            then()
         yield
         for k in (1, 3, 2):
             gather_wait(p, b, buf.at[chunk(0, lax.rem(z + 4 - k, 4))], k)
@@ -198,20 +200,29 @@
         for r in (1, 2, 3):
             att[b, r].wait_recv()
         heads[b] = jnp.concatenate([attn_ref[rows_of(b, 0), :]] + [att_rcv[b, r] for r in range(3)], axis=1)
-        once("wo", local[2].wait, local[3].wait, to_core[0].wait_recv, to_core[1].wait_recv)
-        total = yield from reduce_scatter(0, b, dot_nn(heads[b], wo4[...]))
+        if b == 0:
+            once(local[2].wait, local[3].wait, *[copy.wait_recv for copy in wo_copies])
+        partial = dot_nn(heads[b], wo4[...])
+        total = yield from reduce_scatter(0, b, partial, (lambda: send_weight("cq", 3)) if b == 1 else None)
         local[b].wait()
         resid = x_buf[b].astype(F32) + total
         h_buf[0, b, chunk(0, z)] = rms_norm(resid, nc_ref[...])
         yield from gather(0, b)
-        once("cq", local[4].wait, local[5].wait, to_core[2].wait_recv, to_core[3].wait_recv)
+        if b == 0:
+            once(local[4].wait, *weight_waits("cq"))
         q4 = dot_nt(h_buf[0, b], cq4[...]).astype(BF16)
         for r in (3, 2, 1):
             q_snd[b, r - 1] = q4[:, r * 64:r * 64 + 64]
             start(q_snd.at[b, r - 1], q_rcv.at[b, c, span(y * 64, 64)], q_ssem.at[b, r - 1], q_rsem.at[b, r - 1], quad[r])
         q_rcv[b, c, span(y * 64, 64)] = q4[:, 0:64]
-        yield
-        once("kv", local[6].wait, local[7].wait)
+        if b == 0:
+            send_weight("co", 3)
+        else:
+            for name in Y_SECOND:
+                send_weight(name, 2)
+        yield
+        if b == 0:
+            once(local[5].wait, local[6].wait)
         for half_id, pieces in ((c, (2,)), (1 - c, (1, 3))):
             for r in pieces:
                 remote(q_snd.at[b, r - 1], q_rcv.at[b, quad_c[r], span(quad_y[r] * 64, 64)], q_ssem.at[b, r - 1], q_rsem.at[b, r - 1], quad[r]).wait_recv()
@@ -219,25 +230,27 @@
             for r in reversed(pieces):
                 start(o_buf.at[b, half_id, span(quad_y[r] * 64, 64)], o_rcv.at[b, r - 1], o_ssem.at[b, r - 1], o_rsem.at[b, r - 1], quad[r])
         if b == 1:
-            start_wd()
+            for name in Y_THIRD:
+                send_weight(name, 2)
+            send_weight("wg", 3)
         yield
         for r in (1, 2, 3):
             remote(o_buf.at[b, quad_c[r], span(quad_y[r] * 64, 64)], o_rcv.at[b, r - 1], o_ssem.at[b, r - 1], o_rsem.at[b, r - 1], quad[r]).wait_recv()
         heads[b] = jnp.concatenate([o_buf[b, c, span(y * 64, 64), :]] + [o_rcv[b, r] for r in range(3)], axis=1)
-        once("co", local[8].wait, local[9].wait, to_core[4].wait_recv, to_core[5].wait_recv)
+        if b == 0:
+            once(local[7].wait, *weight_waits("co"))
         partial = dot_nn(heads[b], co4[...])
-        if b == 1:
-            forward_gate_up()
-        total = yield from reduce_scatter(1, b, partial)
+        total = yield from reduce_scatter(1, b, partial, (lambda: send_weight("wu", 3)) if b == 1 else None)
         resid = resid + total
         h_buf[1, b, chunk(0, z)] = rms_norm(resid, nm_ref[...])
-        yield from gather(1, b)
-        if b == 0:
-            forward_wd()
-        once("gu", local[10].wait, local[11].wait, to_core[6].wait_recv, to_core[7].wait_recv, late["wg"].wait_recv, late["wu"].wait_recv)
+        yield from gather(1, b, (lambda: send_weight("wv", 3)) if b == 1 else None)
+        if b == 0:
+            send_weight("wd", 3)
+            once(*[copy.wait for copy in local[8:]], *weight_waits("wg", "wu", "wv"))
         h = h_buf[1, b]
         act[b] = (gelu_tanh(dot_nt(h, wg4[...])) * dot_nt(h, wu4[...])).astype(BF16)
-        once("wd", local[12].wait, to_core[8].wait_recv, late["wd3"].wait_recv)
+        if b == 0:
+            once(*weight_waits("wd"))
         total = yield from reduce_scatter(2, b, dot_nn(act[b], wd4[...]))
         resid = resid + total
         out_ref[chunk(c * 256 + b * 128 + y * 64, z)] = resid.astype(BF16)
@@ -259,33 +272,28 @@
         copy.wait_send()
 
 
-def tail(x_in, attn, mask_t, ck_t, cv_t, wo, cq_t, co, wg_t, wu_t, wd, woy, cqy_t, coy, nc, nm):
+def tail(x_in, attn, mask_t, ck_t, cv_t, wo, cq_t, co, wg_t, wu_t, wd, woy, nc, nm):
     hbm = pl.BlockSpec(memory_space=pltpu.HBM)
-    anywhere = pl.BlockSpec(memory_space=pl.ANY)
     vmem = pl.BlockSpec(memory_space=pltpu.VMEM)
-    units = wd.shape[0]
+    units, wide = wd.shape
+    deep = wo.shape[0]
     dma = pltpu.SemaphoreType.DMA
-    quarter = (256, 1024)
-    scratch = [
-        pltpu.VMEM((2, 16, 1024), BF16), pltpu.VMEM(ck_t.shape, BF16), pltpu.VMEM(cv_t.shape, BF16),
-        pltpu.VMEM(quarter, BF16), pltpu.VMEM(quarter, BF16), pltpu.VMEM(quarter, BF16),
-        pltpu.VMEM((4 * units, 1024), BF16), pltpu.VMEM((4 * units, 1024), BF16), pltpu.VMEM((4 * units, 1024), BF16),
-        pltpu.VMEM((2, 3, 64, 64), BF16), pltpu.VMEM((2, 64, 256), BF16), pltpu.VMEM((2, 3, 64, 64), BF16), pltpu.VMEM((2, 2, 128, 64), BF16),
-        pltpu.VMEM((2, 2, 128, 64), BF16), pltpu.VMEM((2, 3, 64, 64), BF16), pltpu.VMEM((64, 128), F32),
-        pltpu.VMEM((2, 64, 1024), F32), pltpu.VMEM((3, 2, 64, 1024), BF16), pltpu.VMEM((3, 2, 3, 16, 1024), BF16), pltpu.VMEM((2, 2, 64, 1024), BF16),
-        pltpu.VMEM((2, 64, 4 * units), BF16),
-        dma((13,)), dma((15,)), dma((15,)), dma((2, 3)), dma((2, 3)), dma((2, 3)), dma((2, 3)), dma((2, 3)), dma((2, 3)),
-        dma((3, 2, 3)), dma((3, 2, 3)), dma((3, 2, 3)), dma((3, 2, 3)), dma((2, 4)), dma((2, 4)), dma((2, 8)), dma((2, 8)),
-    ]
+    bf16_shapes = [(2, 16, wide), ck_t.shape, cv_t.shape] + [(4 * deep, wide)] * 3 + [(4 * units, wide)] * 3
+    bf16_shapes += [(2, 3, 64, deep), (2, 64, 4 * deep), (2, 3, 64, deep), (2, 2, 128, deep), (2, 2, 128, deep), (2, 3, 64, deep)]
+    z_shapes = [(3, 2, 64, wide), (3, 2, 3, 16, wide), (2, 2, 64, wide), (2, 64, 4 * units)]
+    sems = [(11,), (2,), (2,), (6, 3), (6, 3)] + [(2, 3)] * 6 + [(3, 2, 3)] * 4 + [(2, 4)] * 2 + [(2, 8)] * 2
+    scratch = [pltpu.VMEM(shape, BF16) for shape in bf16_shapes]
+    scratch += [pltpu.VMEM((deep, 128), F32), pltpu.VMEM((2, 64, wide), F32)]
+    scratch += [pltpu.VMEM(shape, BF16) for shape in z_shapes] + [dma(shape) for shape in sems]
     return pl.pallas_call(
         tail_kernel,
         out_shape=jax.ShapeDtypeStruct(x_in.shape, BF16),
-        in_specs=[hbm, vmem, vmem] + [hbm] * 8 + [anywhere] * 3 + [vmem, vmem],
+        in_specs=[hbm, vmem, vmem, hbm, hbm, vmem] + [hbm] * 6 + [vmem, vmem],
         out_specs=vmem,
         scratch_shapes=scratch,
-        compiler_params=pltpu.CompilerParams(collective_id=0, has_side_effects=True, vmem_limit_bytes=60 * 1024 * 1024),
+        compiler_params=pltpu.CompilerParams(collective_id=0, has_side_effects=True, vmem_limit_bytes=VMEM_BYTES),
         name="tail",
-    )(x_in, attn, mask_t, ck_t, cv_t, wo, cq_t, co, wg_t, wu_t, wd, woy, cqy_t, coy, nc, nm)
+    )(x_in, attn, mask_t, ck_t, cv_t, wo, cq_t, co, wg_t, wu_t, wd, woy, nc, nm)
 
 
 def head_kernel(tok_ref, rb_ref, x_ref, wq_ref, wk_ref, wv_ref, ns_ref, k_hbm, v_hbm,
@@ -387,8 +395,8 @@
             pltpu.VMEM((rows, 2 * depth), F32), pltpu.VMEM((rows // 128, depth, 128), F32), pltpu.VMEM((rows // 128, depth, 128), F32),
             pltpu.VMEM((t_len, t_len), F32), dma((2, n_chunks)), dma((2, n_chunks)),
         ],
-        compiler_params=pltpu.CompilerParams(vmem_limit_bytes=60 * 1024 * 1024),
-        cost_estimate=pl.CostEstimate(flops=4 * 10**9, bytes_accessed=34 * 1024 * 1024, transcendentals=65536),
+        compiler_params=pltpu.CompilerParams(vmem_limit_bytes=VMEM_BYTES),
+        cost_estimate=pl.CostEstimate(flops=4 * 10**9, bytes_accessed=34 * 2**20, transcendentals=2**16),
         name="head",
     )(tok_pos, rel_bias, x_in, wq_t, wk_t, wv_t, ns, k_t, v_t)
 
@@ -402,11 +410,8 @@
         new_self_v = jnp.transpose(new_v, (0, 2, 1))[:, :, None, :]
         ck_t = jnp.transpose(cross_k[:, :, 0, :], (1, 2, 0))
         cv_t = jnp.transpose(cross_v[:, :, 0, :], (1, 2, 0))
-        tp_size = mesh.shape["tp"]
-        across_y = [(i, i ^ 2) for i in range(tp_size)]
-        wo_y, cq_y, co_y = (lax.ppermute(w, "tp", across_y) for w in (w_o, cross_q.T, cross_o))
-        out = tail(x_in, attn, enc_mask.T, ck_t, cv_t, w_o, cross_q.T, cross_o, w_gate.T, w_up.T, w_down, wo_y, cq_y, co_y,
-                   norm_cross, norm_mlp)
+        wo_y = lax.ppermute(w_o, "tp", [(i, i ^ 2) for i in range(mesh.shape["tp"])])
+        out = tail(x_in, attn, enc_mask.T, ck_t, cv_t, w_o, cross_q.T, cross_o, w_gate.T, w_up.T, w_down, wo_y, norm_cross, norm_mlp)
         return out, new_self_k, new_self_v
 
     cache_spec = P('dp', None, 'tp', None)

time: 86.1 us -> 86.5 us (level)
  Pallas kernels: 77.1 us -> 79.6 us
  starting transfers between devices: 5.12 us -> 3.09 us
    pallas_call x1, Pallas kernels: 61.9 us -> 64.4 us  [tail(): pl.pallas_call(tail_kernel, out_shape=jax.ShapeDtypeStruct(x_in.shape, BF...]
    ppermute x3 -> x1, starting transfers between devices: 5.12 us -> 3.09 us  [local_layer(): lax.ppermute(w_o, 'tp', [(i, i ^ 2) for i in range(mesh.shape['tp'])])]
    unnamed x7 -> x3, local copies, waits for them, and re-layouts: 2.99 us -> 2.91 us
  transfers between devices with their start and end apart: 3 -> 1, of which waited for: 0 -> 0; matrix products, arithmetic and copies ran while one was open for 0% -> 0% of each run, Pallas kernels for 18% -> 18%
where the time goes in v5:
time: 86.5 us; the launch traced here: 86.3 us
  Pallas kernels  79.6 us (92%)
  starting transfers between devices  3.09 us (4%)
  local copies, waits for them, and re-layouts  2.91 us (3%)
    pallas_call x1, Pallas kernels, tail(): pl.pallas_call(tail_kernel, out_shape=jax.ShapeDtypeStruct(x_in.shape, BF...  64.4 us
    pallas_call x1, Pallas kernels, head(): pl.pallas_call(head_kernel, out_shape=(jax.ShapeDtypeStruct((rows, depth)...  15.2 us
    ppermute x1, starting transfers between devices, local_layer(): lax.ppermute(w_o, 'tp', [(i, i ^ 2) for i in range(mesh.shape['tp'])])  3.09 us
    unnamed x3, local copies, waits for them, and re-layouts  2.91 us
  transfers between devices with their start and end apart: 1, of which 0 were waited for; matrix products, arithmetic and copies ran while one was open for 0% of the time, Pallas kernels for 18%

profile of v5, /device:TPU:0, one launch (start us, length us, event | category | flops | bytes accessed | tf_op | source)
XLA Modules:
  0.0 86.3 jit_solution(14302651873347705816)
XLA Ops:
  0.6 3.1 %collective-permute-start = (bf16[64,1024]{1,0:T(8,128)(2,1)}, bf16[64,1024]{1,0:T(8,128)(2,1)S(1)}, u32[]{:S(2)}, u32[]{:S(2)}) collective-permute-start(bf16[64,1024]{1,0:T(8,128)(2,1)} %wo_ref.1), channel_id=1, source_target_pairs={{0,2},{1,3},{2,0},{3,1},{4,6},{5,7},{6,4},{7,5},{8,10},{9,11},{10,... | collective-permute-start | bytes 393224 | tf_op jit(solution)/shard_map/ppermute | solution.py:413
  3.7 15.2 %head.1 = (bf16[512,64]{1,0:T(8,128)(2,1)}, bf16[512,64,128]{2,1,0:T(8,128)(2,1)}, bf16[512,64,128]{2,1,0:T(8,128)(2,1)}) custom-call(s32[512]{0:T(512)} %tok_ref.1, f32[32]{0:T(128)} %bitcast.41, bf16[512,1024]{1,0:T(8,128)(2,1)} %x_hbm.1, bf16[64,1024]{1,0:T(8,128)(2,1)} %bitcast.36, bf16[64,1024]{1,0:T(8,128)(2,1)} %bitcast.37, ...), custom_call_target="tpu_custom_call" | custom-call | flops 4000000000 | bytes 35651584 | tf_op jit(solution)/shard_map/head/pallas_call | solution.py:388
  18.9 0.0 collective-permute-done.woy_hbm
  19.0 0.0 copy-start
  19.0 0.6 copy-done
  19.6 64.4 %tail.1 = bf16[512,1024]{1,0:T(8,128)(2,1)} custom-call(bf16[512,1024]{1,0:T(8,128)(2,1)} %x_hbm.1, bf16[512,64]{1,0:T(8,128)(2,1)} %get-tuple-element.6.attn_ref, s32[64,512]{1,0:T(8,128)} %bitcast.39, bf16[64,64,512]{2,1,0:T(8,128)(2,1)} %bitcast.32, bf16[64,64,512]{2,1,0:T(8,128)(2,1)} %bitcast.33, bf16[64,1024]{1,0:T(8,128)(2,1)} %wo_ref.1, ...), custom_call_target="tpu_custom_call" | custom-call | tf_op jit(solution)/shard_map/tail/pallas_call | solution.py:288
  84.0 2.3 %copy.26 = bf16[512,1024]{1,0:T(8,128)(2,1)} copy(bf16[512,1024]{1,0:T(8,128)(2,1)} %tail.1) | data formatting | bytes 2097152
Async XLA Ops:
  0.6 18.3 %collective-permute-start = (bf16[64,1024]{1,0:T(8,128)(2,1)}, bf16[64,1024]{1,0:T(8,128)(2,1)S(1)}, u32[]{:S(2)}, u32[]{:S(2)}) collective-permute-start(bf16[64,1024]{1,0:T(8,128)(2,1)} %wo_ref.1), channel_id=1, source_target_pairs={{0,2},{1,3},{2,0},{3,1},{4,6},{5,7},{6,4},{7,5},{8,10},{9,11},{10,... | collective-permute-start | bytes 393224 | tf_op jit(solution)/shard_map/ppermute | solution.py:413
  19.0 0.7 copy-start

commit v6 on v5

--- a/solution.py
+++ b/solution.py
@@ -291,7 +291,7 @@
         in_specs=[hbm, vmem, vmem, hbm, hbm, vmem] + [hbm] * 6 + [vmem, vmem],
         out_specs=vmem,
         scratch_shapes=scratch,
-        compiler_params=pltpu.CompilerParams(collective_id=0, has_side_effects=True, vmem_limit_bytes=VMEM_BYTES),
+        compiler_params=pltpu.CompilerParams(collective_id=0, has_side_effects=True, vmem_limit_bytes=50 * 2**20),
         name="tail",
     )(x_in, attn, mask_t, ck_t, cv_t, wo, cq_t, co, wg_t, wu_t, wd, woy, nc, nm)
 

time: 86.5 us -> 84.7 us (0.979)
  Pallas kernels: 79.6 us -> 78.5 us
  local copies, waits for them, and re-layouts: 2.91 us -> 1.91 us
    pallas_call x1, Pallas kernels: 64.4 us -> 63.2 us  [tail(): pl.pallas_call(tail_kernel, out_shape=jax.ShapeDtypeStruct(x_in.shape, BF...]
    unnamed x3 -> x23, local copies, waits for them, and re-layouts: 2.91 us -> 1.91 us
where the time goes in v6:
time: 84.7 us; the launch traced here: 84.3 us
  Pallas kernels  78.5 us (93%)
  starting transfers between devices  3.09 us (4%)
  local copies, waits for them, and re-layouts  1.91 us (2%)
    pallas_call x1, Pallas kernels, tail(): pl.pallas_call(tail_kernel, out_shape=jax.ShapeDtypeStruct(x_in.shape, BF...  63.2 us
    pallas_call x1, Pallas kernels, head(): pl.pallas_call(head_kernel, out_shape=(jax.ShapeDtypeStruct((rows, depth)...  15.4 us
    ppermute x1, starting transfers between devices, local_layer(): lax.ppermute(w_o, 'tp', [(i, i ^ 2) for i in range(mesh.shape['tp'])])  3.09 us
    unnamed x23, local copies, waits for them, and re-layouts  1.91 us
  transfers between devices with their start and end apart: 1, of which 0 were waited for; matrix products, arithmetic and copies ran while one was open for 0% of the time, Pallas kernels for 18%

profile of v6, /device:TPU:0, one launch (start us, length us, event | category | flops | bytes accessed | tf_op | source)
XLA Modules:
  0.0 84.3 jit_solution(9359481605120744539)
XLA Ops:
  0.6 3.1 %collective-permute-start = (bf16[64,1024]{1,0:T(8,128)(2,1)}, bf16[64,1024]{1,0:T(8,128)(2,1)S(1)}, u32[]{:S(2)}, u32[]{:S(2)}) collective-permute-start(bf16[64,1024]{1,0:T(8,128)(2,1)} %wo_ref.1), channel_id=1, source_target_pairs={{0,2},{1,3},{2,0},{3,1},{4,6},{5,7},{6,4},{7,5},{8,10},{9,11},{10,... | collective-permute-start | bytes 393224 | tf_op jit(solution)/shard_map/ppermute | solution.py:413
  3.7 0.0 copy-start
  3.7 0.0 copy-start.1
  3.7 0.0 copy-start.2
  3.7 0.0 copy-start.3
  3.7 0.0 copy-start.4
  3.7 0.0 copy-start.5
  3.8 0.0 copy-start.6
  3.8 0.0 copy-start.7
  3.8 0.0 copy-start.9
  3.8 0.0 copy-start.10
  3.8 15.4 %head.1 = (bf16[512,64]{1,0:T(8,128)(2,1)}, bf16[512,64,128]{2,1,0:T(8,128)(2,1)}, bf16[512,64,128]{2,1,0:T(8,128)(2,1)}) custom-call(s32[512]{0:T(512)} %tok_ref.1, f32[32]{0:T(128)} %bitcast.41, bf16[512,1024]{1,0:T(8,128)(2,1)} %x_hbm.1, bf16[64,1024]{1,0:T(8,128)(2,1)} %bitcast.38, bf16[64,1024]{1,0:T(8,128)(2,1)} %bitcast.39, ...), custom_call_target="tpu_custom_call" | custom-call | flops 4000000000 | bytes 35651584 | tf_op jit(solution)/shard_map/head/pallas_call | solution.py:388
  19.2 0.0 collective-permute-done.woy_hbm
  19.2 0.0 copy-done
  19.2 0.0 copy-done.1
  19.2 0.0 copy-done.2
  19.2 0.0 copy-done.3
  19.2 0.0 copy-done.4
  19.2 0.0 copy-done.5
  19.2 0.0 copy-done.6
  19.2 0.0 copy-done.7
  19.3 0.0 copy-done.9
  19.3 0.0 copy-done.10
  19.3 0.0 copy-start.8
  19.3 0.9 %copy-done.8 = bf16[512,64]{1,0:T(8,128)(2,1)S(1)} copy-done((bf16[512,64]{1,0:T(8,128)(2,1)S(1)}, bf16[512,64]{1,0:T(8,128)(2,1)}, u32[]{:S(2)}) %copy-start.8) | copy-done | bytes 65560
  20.2 63.2 %tail.1 = bf16[512,1024]{1,0:T(8,128)(2,1)S(1)} custom-call(bf16[512,1024]{1,0:T(8,128)(2,1)S(1)} %copy-done, bf16[512,64]{1,0:T(8,128)(2,1)S(1)} %copy-done.8, s32[64,512]{1,0:T(8,128)S(1)} %bitcast.32, bf16[64,64,512]{2,1,0:T(8,128)(2,1)} %bitcast.36, bf16[64,64,512]{2,1,0:T(8,128)(2,1)} %bitcast.37, bf16[64,1024]{1,0:T(8,128)(2,1)S(1)} %copy-done.5, ...), custom_call_target="tpu_custom_call" | custom-call | tf_op jit(solution)/shard_map/tail/pallas_call | solution.py:288
  83.4 1.0 %copy.26 = bf16[512,1024]{1,0:T(8,128)(2,1)} copy(bf16[512,1024]{1,0:T(8,128)(2,1)S(1)} %tail.1) | data formatting | bytes 2097152
Async XLA Ops:
  0.6 18.5 %collective-permute-start = (bf16[64,1024]{1,0:T(8,128)(2,1)}, bf16[64,1024]{1,0:T(8,128)(2,1)S(1)}, u32[]{:S(2)}, u32[]{:S(2)}) collective-permute-start(bf16[64,1024]{1,0:T(8,128)(2,1)} %wo_ref.1), channel_id=1, source_target_pairs={{0,2},{1,3},{2,0},{3,1},{4,6},{5,7},{6,4},{7,5},{8,10},{9,11},{10,... | collective-permute-start | bytes 393224 | tf_op jit(solution)/shard_map/ppermute | solution.py:413
  3.7 15.5 %copy-start = (bf16[512,1024]{1,0:T(8,128)(2,1)S(1)}, bf16[512,1024]{1,0:T(8,128)(2,1)}, u32[]{:S(2)}) copy-start(bf16[512,1024]{1,0:T(8,128)(2,1)} %x_hbm.1) | copy-start | bytes 3145732
  3.7 15.5 %copy-start.1 = (bf16[1024,176]{0,1:T(8,128)(2,1)S(1)}, bf16[1024,176]{0,1:T(8,128)(2,1)}, u32[]{:S(2)}) copy-start(bf16[1024,176]{0,1:T(8,128)(2,1)} %param.34) | copy-start | bytes 1081348
  3.7 15.5 %copy-start.2 = (bf16[1024,176]{0,1:T(8,128)(2,1)S(1)}, bf16[1024,176]{0,1:T(8,128)(2,1)}, u32[]{:S(2)}) copy-start(bf16[1024,176]{0,1:T(8,128)(2,1)} %param.35) | copy-start | bytes 1081348
  3.7 15.5 %copy-start.3 = (bf16[176,1024]{1,0:T(8,128)(2,1)S(1)}, bf16[176,1024]{1,0:T(8,128)(2,1)}, u32[]{:S(2)}) copy-start(bf16[176,1024]{1,0:T(8,128)(2,1)} %wd_hbm.1) | copy-start | bytes 1081348
  3.7 15.5 %copy-start.4 = (s32[512,64]{0,1:T(8,128)S(1)}, s32[512,64]{0,1:T(8,128)}, u32[]{:S(2)}) copy-start(s32[512,64]{0,1:T(8,128)} %param.26) | copy-start | bytes 393220
  3.7 15.5 %copy-start.5 = (bf16[64,1024]{1,0:T(8,128)(2,1)S(1)}, bf16[64,1024]{1,0:T(8,128)(2,1)}, u32[]{:S(2)}) copy-start(bf16[64,1024]{1,0:T(8,128)(2,1)} %wo_ref.1) | copy-start | bytes 393220
  3.8 15.5 %copy-start.6 = (bf16[1024,64]{0,1:T(8,128)(2,1)S(1)}, bf16[1024,64]{0,1:T(8,128)(2,1)}, u32[]{:S(2)}) copy-start(bf16[1024,64]{0,1:T(8,128)(2,1)} %param.32) | copy-start | bytes 393220
  3.8 15.5 %copy-start.7 = (bf16[64,1024]{1,0:T(8,128)(2,1)S(1)}, bf16[64,1024]{1,0:T(8,128)(2,1)}, u32[]{:S(2)}) copy-start(bf16[64,1024]{1,0:T(8,128)(2,1)} %co_hbm.1) | copy-start | bytes 393220
  3.8 15.5 %copy-start.9 = (bf16[1024]{0:T(1024)(128)(2,1)S(1)}, bf16[1024]{0:T(1024)(128)(2,1)}, u32[]{:S(2)}) copy-start(bf16[1024]{0:T(1024)(128)(2,1)} %nc_ref.1) | copy-start | bytes 6148
  3.8 15.5 %copy-start.10 = (bf16[1024]{0:T(1024)(128)(2,1)S(1)}, bf16[1024]{0:T(1024)(128)(2,1)}, u32[]{:S(2)}) copy-start(bf16[1024]{0:T(1024)(128)(2,1)} %nm_ref.1) | copy-start | bytes 6148
  19.3 0.9 %copy-start.8 = (bf16[512,64]{1,0:T(8,128)(2,1)S(1)}, bf16[512,64]{1,0:T(8,128)(2,1)}, u32[]{:S(2)}) copy-start(bf16[512,64]{1,0:T(8,128)(2,1)} %get-tuple-element.6.attn_ref) | copy-start | bytes 196612

commit v7 on v6

--- a/solution.py
+++ b/solution.py
@@ -11,7 +11,7 @@
 MESH = pl.DeviceIdType.MESH
 F32 = jnp.float32
 BF16 = jnp.bfloat16
-K_ORDER = (2, 1, 3)
+K_ORDER = (3, 2, 1)
 Y_FIRST, Y_SECOND, Y_THIRD = ("cq", "co", "wg"), ("wu",), ("wv", "wd")
 VMEM_BYTES = 60 * 1024 * 1024
 
@@ -338,9 +338,7 @@
     def step(i, carry):
         chunk_copy(i, 0).wait()
         chunk_copy(i, 1).wait()
-        shift = lax.rem(i, 2) * size
-        k_cols = pltpu.roll(k_new[i // 2], shift, 1)
-        v_cols = pltpu.roll(v_new[i // 2], shift, 1)
+        k_cols, v_cols = k_new[i], v_new[i]
         scores = []
         for g in range(size // 8):
             k8, bias8 = [], []
@@ -349,8 +347,8 @@
                 pos = tok_ref[b]
                 at_pos = lane == pos
                 col = g * 8 + j
-                k_b = jnp.where(at_pos, jnp.broadcast_to(k_cols[:, col:col + 1], (depth, t_len)), kbuf[b].astype(F32)).astype(BF16)
-                v_b = jnp.where(at_pos, jnp.broadcast_to(v_cols[:, col:col + 1], (depth, t_len)), vbuf[b].astype(F32)).astype(BF16)
+                k_b = jnp.where(at_pos, pltpu.roll(k_cols, pos + (t_len - col), 1), kbuf[b].astype(F32)).astype(BF16)
+                v_b = jnp.where(at_pos, pltpu.roll(v_cols, pos + (t_len - col), 1), vbuf[b].astype(F32)).astype(BF16)
                 kbuf[b] = k_b
                 vbuf[b] = v_b
                 k8.append(k_b)
@@ -384,7 +382,7 @@
     smem = pl.BlockSpec(memory_space=pltpu.SMEM)
     rows, depth, t_len = k_t.shape
     dma = pltpu.SemaphoreType.DMA
-    n_chunks = 8
+    n_chunks = 4
     return pl.pallas_call(
         head_kernel,
         out_shape=(jax.ShapeDtypeStruct((rows, depth), BF16), jax.ShapeDtypeStruct(k_t.shape, BF16), jax.ShapeDtypeStruct(v_t.shape, BF16)),

time: 84.7 us -> 82.7 us (0.976)
  Pallas kernels: 78.5 us -> 76.1 us
    pallas_call x1, Pallas kernels: 63.2 us -> 61.9 us  [tail(): pl.pallas_call(tail_kernel, out_shape=jax.ShapeDtypeStruct(x_in.shape, BF...]
    pallas_call x1, Pallas kernels: 15.4 us -> 14.2 us  [head(): pl.pallas_call(head_kernel, out_shape=(jax.ShapeDtypeStruct((rows, depth)...]
  transfers between devices with their start and end apart: 1 -> 1, of which waited for: 0 -> 0; matrix products, arithmetic and copies ran while one was open for 0% -> 0% of each run, Pallas kernels for 18% -> 17%
where the time goes in v7:
time: 82.7 us; the launch traced here: 81.9 us
  Pallas kernels  76.1 us (92%)
  starting transfers between devices  3.09 us (4%)
  local copies, waits for them, and re-layouts  1.91 us (2%)
    pallas_call x1, Pallas kernels, tail(): pl.pallas_call(tail_kernel, out_shape=jax.ShapeDtypeStruct(x_in.shape, BF...  61.9 us
    pallas_call x1, Pallas kernels, head(): pl.pallas_call(head_kernel, out_shape=(jax.ShapeDtypeStruct((rows, depth)...  14.2 us
    ppermute x1, starting transfers between devices, local_layer(): lax.ppermute(w_o, 'tp', [(i, i ^ 2) for i in range(mesh.shape['tp'])])  3.09 us
    unnamed x23, local copies, waits for them, and re-layouts  1.91 us
  transfers between devices with their start and end apart: 1, of which 0 were waited for; matrix products, arithmetic and copies ran while one was open for 0% of the time, Pallas kernels for 17%

profile of v7, /device:TPU:0, one launch (start us, length us, event | category | flops | bytes accessed | tf_op | source)
XLA Modules:
  0.0 81.9 jit_solution(2671419967360208885)
XLA Ops:
  0.6 3.1 %collective-permute-start = (bf16[64,1024]{1,0:T(8,128)(2,1)}, bf16[64,1024]{1,0:T(8,128)(2,1)S(1)}, u32[]{:S(2)}, u32[]{:S(2)}) collective-permute-start(bf16[64,1024]{1,0:T(8,128)(2,1)} %wo_ref.1), channel_id=1, source_target_pairs={{0,2},{1,3},{2,0},{3,1},{4,6},{5,7},{6,4},{7,5},{8,10},{9,11},{10,... | collective-permute-start | bytes 393224 | tf_op jit(solution)/shard_map/ppermute | solution.py:411
  3.7 0.0 copy-start
  3.7 0.0 copy-start.1
  3.7 0.0 copy-start.2
  3.7 0.0 copy-start.3
  3.7 0.0 copy-start.4
  3.7 0.0 copy-start.5
  3.8 0.0 copy-start.6
  3.8 0.0 copy-start.7
  3.8 0.0 copy-start.9
  3.8 0.0 copy-start.10
  3.8 14.2 %head.1 = (bf16[512,64]{1,0:T(8,128)(2,1)}, bf16[512,64,128]{2,1,0:T(8,128)(2,1)}, bf16[512,64,128]{2,1,0:T(8,128)(2,1)}) custom-call(s32[512]{0:T(512)} %tok_ref.1, f32[32]{0:T(128)} %bitcast.41, bf16[512,1024]{1,0:T(8,128)(2,1)} %x_hbm.1, bf16[64,1024]{1,0:T(8,128)(2,1)} %bitcast.38, bf16[64,1024]{1,0:T(8,128)(2,1)} %bitcast.39, ...), custom_call_target="tpu_custom_call" | custom-call | flops 4000000000 | bytes 35651584 | tf_op jit(solution)/shard_map/head/pallas_call | solution.py:386
  18.0 0.0 collective-permute-done.woy_hbm
  18.0 0.0 copy-done
  18.0 0.0 copy-done.1
  18.0 0.0 copy-done.2
  18.0 0.0 copy-done.3
  18.0 0.0 copy-done.4
  18.1 0.0 copy-done.5
  18.1 0.0 copy-done.6
  18.1 0.0 copy-done.7
  18.1 0.0 copy-done.9
  18.1 0.0 copy-done.10
  18.1 0.0 copy-start.8
  18.1 0.9 %copy-done.8 = bf16[512,64]{1,0:T(8,128)(2,1)S(1)} copy-done((bf16[512,64]{1,0:T(8,128)(2,1)S(1)}, bf16[512,64]{1,0:T(8,128)(2,1)}, u32[]{:S(2)}) %copy-start.8) | copy-done | bytes 65560
  19.0 61.9 %tail.1 = bf16[512,1024]{1,0:T(8,128)(2,1)S(1)} custom-call(bf16[512,1024]{1,0:T(8,128)(2,1)S(1)} %copy-done, bf16[512,64]{1,0:T(8,128)(2,1)S(1)} %copy-done.8, s32[64,512]{1,0:T(8,128)S(1)} %bitcast.32, bf16[64,64,512]{2,1,0:T(8,128)(2,1)} %bitcast.36, bf16[64,64,512]{2,1,0:T(8,128)(2,1)} %bitcast.37, bf16[64,1024]{1,0:T(8,128)(2,1)S(1)} %copy-done.5, ...), custom_call_target="tpu_custom_call" | custom-call | tf_op jit(solution)/shard_map/tail/pallas_call | solution.py:288
  80.9 1.0 %copy.26 = bf16[512,1024]{1,0:T(8,128)(2,1)} copy(bf16[512,1024]{1,0:T(8,128)(2,1)S(1)} %tail.1) | data formatting | bytes 2097152
Async XLA Ops:
  0.6 17.4 %collective-permute-start = (bf16[64,1024]{1,0:T(8,128)(2,1)}, bf16[64,1024]{1,0:T(8,128)(2,1)S(1)}, u32[]{:S(2)}, u32[]{:S(2)}) collective-permute-start(bf16[64,1024]{1,0:T(8,128)(2,1)} %wo_ref.1), channel_id=1, source_target_pairs={{0,2},{1,3},{2,0},{3,1},{4,6},{5,7},{6,4},{7,5},{8,10},{9,11},{10,... | collective-permute-start | bytes 393224 | tf_op jit(solution)/shard_map/ppermute | solution.py:411
  3.7 14.3 %copy-start = (bf16[512,1024]{1,0:T(8,128)(2,1)S(1)}, bf16[512,1024]{1,0:T(8,128)(2,1)}, u32[]{:S(2)}) copy-start(bf16[512,1024]{1,0:T(8,128)(2,1)} %x_hbm.1) | copy-start | bytes 3145732
  3.7 14.3 %copy-start.1 = (bf16[1024,176]{0,1:T(8,128)(2,1)S(1)}, bf16[1024,176]{0,1:T(8,128)(2,1)}, u32[]{:S(2)}) copy-start(bf16[1024,176]{0,1:T(8,128)(2,1)} %param.34) | copy-start | bytes 1081348
  3.7 14.3 %copy-start.2 = (bf16[1024,176]{0,1:T(8,128)(2,1)S(1)}, bf16[1024,176]{0,1:T(8,128)(2,1)}, u32[]{:S(2)}) copy-start(bf16[1024,176]{0,1:T(8,128)(2,1)} %param.35) | copy-start | bytes 1081348
  3.7 14.3 %copy-start.3 = (bf16[176,1024]{1,0:T(8,128)(2,1)S(1)}, bf16[176,1024]{1,0:T(8,128)(2,1)}, u32[]{:S(2)}) copy-start(bf16[176,1024]{1,0:T(8,128)(2,1)} %wd_hbm.1) | copy-start | bytes 1081348
  3.7 14.3 %copy-start.4 = (s32[512,64]{0,1:T(8,128)S(1)}, s32[512,64]{0,1:T(8,128)}, u32[]{:S(2)}) copy-start(s32[512,64]{0,1:T(8,128)} %param.26) | copy-start | bytes 393220
  3.7 14.3 %copy-start.5 = (bf16[64,1024]{1,0:T(8,128)(2,1)S(1)}, bf16[64,1024]{1,0:T(8,128)(2,1)}, u32[]{:S(2)}) copy-start(bf16[64,1024]{1,0:T(8,128)(2,1)} %wo_ref.1) | copy-start | bytes 393220
  3.8 14.3 %copy-start.6 = (bf16[1024,64]{0,1:T(8,128)(2,1)S(1)}, bf16[1024,64]{0,1:T(8,128)(2,1)}, u32[]{:S(2)}) copy-start(bf16[1024,64]{0,1:T(8,128)(2,1)} %param.32) | copy-start | bytes 393220
  3.8 14.3 %copy-start.7 = (bf16[64,1024]{1,0:T(8,128)(2,1)S(1)}, bf16[64,1024]{1,0:T(8,128)(2,1)}, u32[]{:S(2)}) copy-start(bf16[64,1024]{1,0:T(8,128)(2,1)} %co_hbm.1) | copy-start | bytes 393220
  3.8 14.3 %copy-start.9 = (bf16[1024]{0:T(1024)(128)(2,1)S(1)}, bf16[1024]{0:T(1024)(128)(2,1)}, u32[]{:S(2)}) copy-start(bf16[1024]{0:T(1024)(128)(2,1)} %nc_ref.1) | copy-start | bytes 6148
  3.8 14.3 %copy-start.10 = (bf16[1024]{0:T(1024)(128)(2,1)S(1)}, bf16[1024]{0:T(1024)(128)(2,1)}, u32[]{:S(2)}) copy-start(bf16[1024]{0:T(1024)(128)(2,1)} %nm_ref.1) | copy-start | bytes 6148
  18.1 0.9 %copy-start.8 = (bf16[512,64]{1,0:T(8,128)(2,1)S(1)}, bf16[512,64]{1,0:T(8,128)(2,1)}, u32[]{:S(2)}) copy-start(bf16[512,64]{1,0:T(8,128)(2,1)} %get-tuple-element.6.attn_ref) | copy-start | bytes 196612

commit v8 on v7

--- a/solution.py
+++ b/solution.py
@@ -134,7 +134,7 @@
         return total
 
     def gather_start(p, b, mine):
-        for k in K_ORDER:
+        for k in (2, 1, 3):
             start(mine, mine, gzs_sem.at[p, b, k - 1], gzr_sem.at[p, b, k - 1], z_peer[k])
 
     def gather_wait(p, b, part, k):

time: 82.7 us -> 81.8 us (0.989)
  Pallas kernels: 76.1 us -> 75.2 us
    pallas_call x1, Pallas kernels: 61.9 us -> 61 us  [tail(): pl.pallas_call(tail_kernel, out_shape=jax.ShapeDtypeStruct(x_in.shape, BF...]
  transfers between devices with their start and end apart: 1 -> 1, of which waited for: 0 -> 0; matrix products, arithmetic and copies ran while one was open for 0% -> 0% of each run, Pallas kernels for 17% -> 18%
where the time goes in v8:
time: 81.8 us; the launch traced here: 81 us
  Pallas kernels  75.2 us (92%)
  starting transfers between devices  3.09 us (4%)
  local copies, waits for them, and re-layouts  1.91 us (2%)
    pallas_call x1, Pallas kernels, tail(): pl.pallas_call(tail_kernel, out_shape=jax.ShapeDtypeStruct(x_in.shape, BF...  61 us
    pallas_call x1, Pallas kernels, head(): pl.pallas_call(head_kernel, out_shape=(jax.ShapeDtypeStruct((rows, depth)...  14.2 us
    ppermute x1, starting transfers between devices, local_layer(): lax.ppermute(w_o, 'tp', [(i, i ^ 2) for i in range(mesh.shape['tp'])])  3.09 us
    unnamed x23, local copies, waits for them, and re-layouts  1.91 us
  transfers between devices with their start and end apart: 1, of which 0 were waited for; matrix products, arithmetic and copies ran while one was open for 0% of the time, Pallas kernels for 18%

profile of v8, /device:TPU:0, one launch (start us, length us, event | category | flops | bytes accessed | tf_op | source)
XLA Modules:
  0.0 81.0 jit_solution(7095732327912592662)
XLA Ops:
  0.6 3.1 %collective-permute-start = (bf16[64,1024]{1,0:T(8,128)(2,1)}, bf16[64,1024]{1,0:T(8,128)(2,1)S(1)}, u32[]{:S(2)}, u32[]{:S(2)}) collective-permute-start(bf16[64,1024]{1,0:T(8,128)(2,1)} %wo_ref.1), channel_id=1, source_target_pairs={{0,2},{1,3},{2,0},{3,1},{4,6},{5,7},{6,4},{7,5},{8,10},{9,11},{10,... | collective-permute-start | bytes 393224 | tf_op jit(solution)/shard_map/ppermute | solution.py:411
  3.7 0.0 copy-start
  3.7 0.0 copy-start.1
  3.7 0.0 copy-start.2
  3.7 0.0 copy-start.3
  3.7 0.0 copy-start.4
  3.7 0.0 copy-start.5
  3.8 0.0 copy-start.6
  3.8 0.0 copy-start.7
  3.8 0.0 copy-start.9
  3.8 0.0 copy-start.10
  3.8 14.2 %head.1 = (bf16[512,64]{1,0:T(8,128)(2,1)}, bf16[512,64,128]{2,1,0:T(8,128)(2,1)}, bf16[512,64,128]{2,1,0:T(8,128)(2,1)}) custom-call(s32[512]{0:T(512)} %tok_ref.1, f32[32]{0:T(128)} %bitcast.41, bf16[512,1024]{1,0:T(8,128)(2,1)} %x_hbm.1, bf16[64,1024]{1,0:T(8,128)(2,1)} %bitcast.38, bf16[64,1024]{1,0:T(8,128)(2,1)} %bitcast.39, ...), custom_call_target="tpu_custom_call" | custom-call | flops 4000000000 | bytes 35651584 | tf_op jit(solution)/shard_map/head/pallas_call | solution.py:386
  18.0 0.0 collective-permute-done.woy_hbm
  18.0 0.0 copy-done
  18.0 0.0 copy-done.1
  18.0 0.0 copy-done.2
  18.0 0.0 copy-done.3
  18.0 0.0 copy-done.4
  18.1 0.0 copy-done.5
  18.1 0.0 copy-done.6
  18.1 0.0 copy-done.7
  18.1 0.0 copy-done.9
  18.1 0.0 copy-done.10
  18.1 0.0 copy-start.8
  18.1 0.9 %copy-done.8 = bf16[512,64]{1,0:T(8,128)(2,1)S(1)} copy-done((bf16[512,64]{1,0:T(8,128)(2,1)S(1)}, bf16[512,64]{1,0:T(8,128)(2,1)}, u32[]{:S(2)}) %copy-start.8) | copy-done | bytes 65560
  19.0 61.0 %tail.1 = bf16[512,1024]{1,0:T(8,128)(2,1)S(1)} custom-call(bf16[512,1024]{1,0:T(8,128)(2,1)S(1)} %copy-done, bf16[512,64]{1,0:T(8,128)(2,1)S(1)} %copy-done.8, s32[64,512]{1,0:T(8,128)S(1)} %bitcast.32, bf16[64,64,512]{2,1,0:T(8,128)(2,1)} %bitcast.36, bf16[64,64,512]{2,1,0:T(8,128)(2,1)} %bitcast.37, bf16[64,1024]{1,0:T(8,128)(2,1)S(1)} %copy-done.5, ...), custom_call_target="tpu_custom_call" | custom-call | tf_op jit(solution)/shard_map/tail/pallas_call | solution.py:288
  80.0 1.0 %copy.26 = bf16[512,1024]{1,0:T(8,128)(2,1)} copy(bf16[512,1024]{1,0:T(8,128)(2,1)S(1)} %tail.1) | data formatting | bytes 2097152
Async XLA Ops:
  0.6 17.4 %collective-permute-start = (bf16[64,1024]{1,0:T(8,128)(2,1)}, bf16[64,1024]{1,0:T(8,128)(2,1)S(1)}, u32[]{:S(2)}, u32[]{:S(2)}) collective-permute-start(bf16[64,1024]{1,0:T(8,128)(2,1)} %wo_ref.1), channel_id=1, source_target_pairs={{0,2},{1,3},{2,0},{3,1},{4,6},{5,7},{6,4},{7,5},{8,10},{9,11},{10,... | collective-permute-start | bytes 393224 | tf_op jit(solution)/shard_map/ppermute | solution.py:411
  3.7 14.3 %copy-start = (bf16[512,1024]{1,0:T(8,128)(2,1)S(1)}, bf16[512,1024]{1,0:T(8,128)(2,1)}, u32[]{:S(2)}) copy-start(bf16[512,1024]{1,0:T(8,128)(2,1)} %x_hbm.1) | copy-start | bytes 3145732
  3.7 14.3 %copy-start.1 = (bf16[1024,176]{0,1:T(8,128)(2,1)S(1)}, bf16[1024,176]{0,1:T(8,128)(2,1)}, u32[]{:S(2)}) copy-start(bf16[1024,176]{0,1:T(8,128)(2,1)} %param.34) | copy-start | bytes 1081348
  3.7 14.3 %copy-start.2 = (bf16[1024,176]{0,1:T(8,128)(2,1)S(1)}, bf16[1024,176]{0,1:T(8,128)(2,1)}, u32[]{:S(2)}) copy-start(bf16[1024,176]{0,1:T(8,128)(2,1)} %param.35) | copy-start | bytes 1081348
  3.7 14.3 %copy-start.3 = (bf16[176,1024]{1,0:T(8,128)(2,1)S(1)}, bf16[176,1024]{1,0:T(8,128)(2,1)}, u32[]{:S(2)}) copy-start(bf16[176,1024]{1,0:T(8,128)(2,1)} %wd_hbm.1) | copy-start | bytes 1081348
  3.7 14.3 %copy-start.4 = (s32[512,64]{0,1:T(8,128)S(1)}, s32[512,64]{0,1:T(8,128)}, u32[]{:S(2)}) copy-start(s32[512,64]{0,1:T(8,128)} %param.26) | copy-start | bytes 393220
  3.7 14.3 %copy-start.5 = (bf16[64,1024]{1,0:T(8,128)(2,1)S(1)}, bf16[64,1024]{1,0:T(8,128)(2,1)}, u32[]{:S(2)}) copy-start(bf16[64,1024]{1,0:T(8,128)(2,1)} %wo_ref.1) | copy-start | bytes 393220
  3.8 14.3 %copy-start.6 = (bf16[1024,64]{0,1:T(8,128)(2,1)S(1)}, bf16[1024,64]{0,1:T(8,128)(2,1)}, u32[]{:S(2)}) copy-start(bf16[1024,64]{0,1:T(8,128)(2,1)} %param.32) | copy-start | bytes 393220
  3.8 14.3 %copy-start.7 = (bf16[64,1024]{1,0:T(8,128)(2,1)S(1)}, bf16[64,1024]{1,0:T(8,128)(2,1)}, u32[]{:S(2)}) copy-start(bf16[64,1024]{1,0:T(8,128)(2,1)} %co_hbm.1) | copy-start | bytes 393220
  3.8 14.3 %copy-start.9 = (bf16[1024]{0:T(1024)(128)(2,1)S(1)}, bf16[1024]{0:T(1024)(128)(2,1)}, u32[]{:S(2)}) copy-start(bf16[1024]{0:T(1024)(128)(2,1)} %nc_ref.1) | copy-start | bytes 6148
  3.8 14.3 %copy-start.10 = (bf16[1024]{0:T(1024)(128)(2,1)S(1)}, bf16[1024]{0:T(1024)(128)(2,1)}, u32[]{:S(2)}) copy-start(bf16[1024]{0:T(1024)(128)(2,1)} %nm_ref.1) | copy-start | bytes 6148
  18.1 0.9 %copy-start.8 = (bf16[512,64]{1,0:T(8,128)(2,1)S(1)}, bf16[512,64]{1,0:T(8,128)(2,1)}, u32[]{:S(2)}) copy-start(bf16[512,64]{1,0:T(8,128)(2,1)} %get-tuple-element.6.attn_ref) | copy-start | bytes 196612
